TPU v7x, 32 devices: a whole 2x2x4 slice. The times are simulated.
32 devices in a mesh: dp: 8 (over y, x, core), tp: 4 (over z).
Axes of the slice: x: 2, y: 2, z: 4, core: 2. Of those that a mesh axis runs over, the one named last changes fastest.
Arguments:
- x_tokens: bfloat16 [8192, 8192], P(('dp', 'tp')), may hold values from -6 to 6
- segment_ids: int32 [8, 1024], P('dp'), may hold values from 0 to 3, never falling along the last dimension, each value on 1 to 512 neighbouring positions
- attended_grad: bfloat16 [8192, 4096], P('dp', 'tp'), may hold values from -6 to 6
- norm_gain: float32 [8192], replicated, may hold values from 0.1 to 1.9
- w_query: bfloat16 [8192, 4096], P(None, 'tp'), may hold values from -1 to 1
- w_key: bfloat16 [8192, 1024], P(None, 'tp'), may hold values from -4 to 4
- w_value: bfloat16 [8192, 1024], P(None, 'tp'), may hold values from -0.0625 to 0.0625
Outputs:
- attended: bfloat16 [8192, 4096], P('dp', 'tp')
- input_grad: bfloat16 [8192, 8192], P(('dp', 'tp'))
- gain_grad: float32 [8192], replicated
- grad_query: float32 [8192, 4096], P('dp', 'tp')
- grad_key: float32 [8192, 1024], P('dp', 'tp')
- grad_value: float32 [8192, 1024], P('dp', 'tp')
Inputs may be any that keep to these rules, and one draw needn't show every extreme that they name: `segment_ids`: along each replica's row the numbers never fall; every number 0 to 3 covers one run of 1 to 512 positions.
All inputs are finite; a program needn't handle non-finite values.
Results may differ from a plain program's by a relative error of at most 0.028.
The roundings to bfloat16 on the way count: a program that leaves them out, or rounds other values in their place, can miss the bound.
Values may be sent and summed in bfloat16 or wider, within the bound.
No kernel may reach another device: no remote copies, remote signals or barrier semaphores. Data moves between devices by JAX's collectives and lax.ppermute only.
A program may use at most 256 MiB of HBM per device.

v0:
```python
import jax
import jax.numpy as jnp
from jax import lax
from jax.sharding import PartitionSpec as P

HD = 128


epsilon = 1e-05
rope_base = 500000.0


def rope_tables(segment_row, head_dim):
    length = segment_row.shape[0]
    earlier = (segment_row[None, :] < segment_row[:, None]).astype(jnp.int32)
    offset = jnp.arange(length, dtype=jnp.int32) - jnp.sum(earlier, axis=1)
    half_dim = head_dim // 2
    inverse_freq = rope_base ** (-(jnp.arange(half_dim, dtype=jnp.float32) * 2.0 / head_dim))
    angle = offset.astype(jnp.float32)[:, None] * inverse_freq[None, :]
    return (jnp.cos(angle)[:, None, :], jnp.sin(angle)[:, None, :])


def attend_mask(segment_row):
    length = segment_row.shape[0]
    position = jnp.arange(length, dtype=jnp.int32)
    return (position[None, :] <= position[:, None]) & (segment_row[None, :] == segment_row[:, None])


def apply_rope(head_rows, cosine_table, sine_table, direction):
    half_dim = head_rows.shape[-1] // 2
    first_half = head_rows[..., :half_dim]
    second_half = head_rows[..., half_dim:]
    return jnp.concatenate(
        [
            first_half * cosine_table - direction * second_half * sine_table,
            second_half * cosine_table + direction * first_half * sine_table,
        ],
        axis=-1,
    )


def contract_first(left, right):
    return lax.dot_general(
        left, right, (((0,), (0,)), ((), ())), preferred_element_type=jnp.float32
    )


def contract_last(left, right):
    return lax.dot_general(
        left, right, (((1,), (1,)), ((), ())), preferred_element_type=jnp.float32
    )


def body(x_tokens, segment_ids, attended_grad, norm_gain, w_query, w_key, w_value):
    head_dim = HD
    q_heads = w_query.shape[1] // head_dim
    kv_heads = w_key.shape[1] // head_dim
    group = q_heads // kv_heads
    score_scale = float(head_dim) ** (-0.5)
    segment_row = segment_ids[0]
    as_float = x_tokens.astype(jnp.float32)
    inverse = lax.rsqrt(jnp.mean(as_float * as_float, axis=1, keepdims=True) + epsilon)
    x_hat = as_float * inverse
    normed = lax.all_gather((x_hat * norm_gain).astype(jnp.bfloat16), "tp", axis=0, tiled=True)
    seq_len = normed.shape[0]
    cosine_table, sine_table = rope_tables(segment_row, head_dim)
    allowed = attend_mask(segment_row)
    query_f = jnp.dot(normed, w_query, preferred_element_type=jnp.float32).reshape(
        seq_len, q_heads, head_dim
    )
    queries = apply_rope(query_f, cosine_table, sine_table, 1.0).astype(jnp.bfloat16)
    key_f = jnp.dot(normed, w_key, preferred_element_type=jnp.float32).reshape(
        seq_len, kv_heads, head_dim
    )
    key_rows = apply_rope(key_f, cosine_table, sine_table, 1.0).astype(jnp.bfloat16)
    values_in = (
        jnp.dot(normed, w_value, preferred_element_type=jnp.float32)
        .astype(jnp.bfloat16)
        .reshape(seq_len, kv_heads, head_dim)
    )
    grouped = queries.reshape(seq_len, kv_heads, group, head_dim)
    out_grouped = attended_grad.reshape(seq_len, kv_heads, group, head_dim)
    block_rows = min(512, seq_len)
    block_count = seq_len // block_rows
    value_total = jnp.zeros((seq_len, kv_heads, head_dim), jnp.float32)
    key_total = jnp.zeros((seq_len, kv_heads, head_dim), jnp.float32)
    attended_parts = []
    query_parts = []
    for block_index in range(block_count):
        first = block_index * block_rows
        last = first + block_rows
        query_block = grouped[first:last]
        keys_seen = key_rows[:last]
        values_seen = values_in[:last]
        mask_block = allowed[first:last, :last]
        scores = (
            jnp.einsum("skgd,tkd->kgst", query_block, keys_seen, preferred_element_type=jnp.float32)
            * score_scale
        )
        scores = jnp.where(mask_block[None, None], scores, -1e30)
        highest = jnp.max(scores, axis=3, keepdims=True)
        exponent = jnp.exp(scores - highest)
        probability = exponent / jnp.sum(exponent, axis=3, keepdims=True)
        weights_b = probability.astype(jnp.bfloat16)
        attended_block = jnp.einsum(
            "kgst,tkd->skgd", weights_b, values_seen, preferred_element_type=jnp.float32
        ).astype(jnp.bfloat16)
        grad_block = out_grouped[first:last]
        row_delta = jnp.sum(
            grad_block.astype(jnp.float32) * attended_block.astype(jnp.float32), axis=3
        )
        value_part = jnp.einsum(
            "kgst,skgd->tkd", weights_b, grad_block, preferred_element_type=jnp.float32
        )
        prob_d = jnp.einsum(
            "skgd,tkd->kgst", grad_block, values_seen, preferred_element_type=jnp.float32
        )
        score_d = (
            probability * (prob_d - jnp.transpose(row_delta, (1, 2, 0))[..., None]) * score_scale
        ).astype(jnp.bfloat16)
        query_parts.append(
            jnp.einsum("kgst,tkd->skgd", score_d, keys_seen, preferred_element_type=jnp.float32)
        )
        key_part = jnp.einsum(
            "kgst,skgd->tkd", score_d, query_block, preferred_element_type=jnp.float32
        )
        padding = ((0, seq_len - last), (0, 0), (0, 0))
        value_total = value_total + jnp.pad(value_part, padding)
        key_total = key_total + jnp.pad(key_part, padding)
        attended_parts.append(attended_block)
    attended = jnp.concatenate(attended_parts, axis=0).reshape(seq_len, q_heads * head_dim)
    query_rot = jnp.concatenate(query_parts, axis=0).reshape(seq_len, q_heads, head_dim)
    query_d = (
        apply_rope(query_rot, cosine_table, sine_table, -1.0)
        .astype(jnp.bfloat16)
        .reshape(seq_len, q_heads * head_dim)
    )
    key_d = (
        apply_rope(key_total, cosine_table, sine_table, -1.0)
        .astype(jnp.bfloat16)
        .reshape(seq_len, kv_heads * head_dim)
    )
    value_flat = value_total.astype(jnp.bfloat16).reshape(seq_len, kv_heads * head_dim)
    total = contract_last(query_d, w_query)
    total = total + contract_last(key_d, w_key)
    normed_d = lax.psum_scatter(
        (total + contract_last(value_flat, w_value)).astype(jnp.bfloat16),
        "tp",
        scatter_dimension=0,
        tiled=True,
    ).astype(jnp.float32)
    scaled_d = normed_d * norm_gain
    input_grad = (
        inverse * (scaled_d - x_hat * jnp.mean(scaled_d * x_hat, axis=1, keepdims=True))
    ).astype(jnp.bfloat16)
    gain_grad = lax.psum(jnp.sum(normed_d * x_hat, axis=0), ("dp", "tp"))
    merged = lax.psum_scatter(
        jnp.concatenate(
            [
                contract_first(normed, query_d),
                contract_first(normed, key_d),
                contract_first(normed, value_flat),
            ],
            axis=1,
        ).astype(jnp.bfloat16),
        "dp",
        scatter_dimension=0,
        tiled=True,
    ).astype(jnp.float32)
    query_cols = query_d.shape[1]
    key_cols = key_d.shape[1]
    grad_query = merged[:, :query_cols]
    grad_key = merged[:, query_cols : query_cols + key_cols]
    grad_value = merged[:, query_cols + key_cols :]
    return (attended, input_grad, gain_grad, grad_query, grad_key, grad_value)


def solution(mesh):
    placed = (
        P(("dp", "tp"), None),
        P("dp", None),
        P("dp", "tp"),
        P(),
        P(None, "tp"),
        P(None, "tp"),
        P(None, "tp"),
    )
    return jax.shard_map(
        body,
        mesh=mesh,
        in_specs=placed,
        out_specs=(
            P("dp", "tp"),
            P(("dp", "tp"), None),
            P(),
            P("dp", "tp"),
            P("dp", "tp"),
            P("dp", "tp"),
        ),
        check_vma=False,
    )
```

profile of v0, /device:TPU:0, one launch (start us, length us, event | category | flops | bytes accessed | tf_op | source)
XLA Modules:
  0.0 944.8 jit_solution(15693421000934270268)
XLA Ops:
  10.9 5.4 fusion.12
  26.1 279.8 %all-gather.2.cloned.1.call-done = bf16[1024,8192]{1,0:T(8,128)(2,1)} async-done(((bf16[256,8192]{1,0:T(8,128)(2,1)}), bf16[1024,8192]{1,0:T(8,128)(2,1)}) %all-gather.2.cloned.1.call-update) | async-done | bytes 16777232 | tf_op jit(solution)/shard_map/all_gather | solution.py:64
  305.9 9.5 %convolution_convert_fusion.5 = bf16[1024,256]{0,1:T(8,128)(2,1)S(1)} fusion(bf16[1024,8192]{1,0:T(8,128)(2,1)} %all-gather.2.cloned.1.call-done, bf16[8192,256]{1,0:T(8,128)(2,1)} %param.13), kind=kOutput, calls=%fused_computation.71 | convolution fusion | flops 4295229440 | bytes 21495808 | tf_op jit(solution)/shard_map/dot_general | solution.py:77
  316.2 8.2 fusion.59
  327.2 23.6 %fusion.60 = f32[1024,1024]{0,1:T(8,128)S(1)} fusion(bf16[1024,8192]{1,0:T(8,128)(2,1)} %all-gather.2.cloned.1.call-done, bf16[8192,1024]{1,0:T(8,128)(2,1)} %param.11), kind=kOutput, calls=%fused_computation.104 | convolution fusion | flops 17179869184 | bytes 37748736 | tf_op jit(solution)/shard_map/dot_general | solution.py:68
  353.5 7.7 fusion.54
  361.2 4.6 fusion.28
  376.0 10.2 %fusion.53 = (f32[2,4,512]{2,1,0:T(4,128)S(1)}, f32[2,4,512,1024]{2,3,1,0:T(8,128)}) fusion(pred[512,1024]{0,1:T(8,128)(4,1)} %slice.106, bf16[512,2,4,128]{0,3,2,1:T(8,128)(2,1)S(1)} %bitcast.187, bf16[1024,2,64]{2,0,1:T(8,128)(2,1)S(1)} %get-tuple-element.33, bf16[1024,2,64]{2,0,1:T(8,128)(2,1)S(1)} %get-tuple-element.32), kind=kOutput, calls=%fused_computation.101 | convolution fusion | flops 1091568640 | bytes 18890752 | tf_op jit(solution)/shard_map/sub | solution.py:102
  386.2 6.9 fusion.22
  395.4 3.6 fusion.35
  399.0 7.3 fusion.4
  417.3 13.2 %fusion.62 = f32[1024,8192]{1,0:T(8,128)} fusion(bf16[1024,256]{0,1:T(8,128)(2,1)S(1)} %bitcast.189, bf16[8192,256]{1,0:T(8,128)(2,1)S(1)} %copy-done.11), kind=kOutput, calls=%fused_computation.106 | convolution fusion | flops 4294967296 | bytes 38273024 | tf_op jit(solution)/shard_map/dot_general | solution.py:49
  430.5 15.5 %fusion.61 = f32[1024,8192]{1,0:T(8,128)} fusion(bf16[1024,256]{0,1:T(8,128)(2,1)S(1)} %bitcast.191, bf16[8192,256]{1,0:T(8,128)(2,1)} %param.12), kind=kOutput, calls=%fused_computation.105 | convolution fusion | flops 4294967296 | bytes 38273024 | tf_op jit(solution)/shard_map/dot_general | solution.py:49
  446.3 36.7 %add_convert_fusion = bf16[1024,8192]{1,0:T(8,128)(2,1)} fusion(f32[1024,8192]{1,0:T(8,128)} %fusion.62, f32[1024,8192]{1,0:T(8,128)} %fusion.61, bf16[1024,1024]{0,1:T(8,128)(2,1)S(1)} %bitcast.193, bf16[8192,1024]{1,0:T(8,128)(2,1)} %param.11), kind=kOutput, calls=%fused_computation.2 | convolution fusion | flops 17205035008 | bytes 102760448 | tf_op jit(solution)/shard_map/dot_general | solution.py:49
  483.1 12.6 %convolution_convert_fusion.2 = bf16[8192,256]{0,1:T(8,128)(2,1)} fusion(bf16[1024,256]{0,1:T(8,128)(2,1)S(1)} %bitcast.192, bf16[1024,8192]{1,0:T(8,128)(2,1)} %all-gather.2.cloned.1.call-done), kind=kOutput, calls=%fused_computation.20 | convolution fusion | flops 4297064448 | bytes 21495808 | tf_op jit(solution)/shard_map/dot_general | solution.py:43
  495.7 11.9 %convolution_convert_fusion.1 = bf16[8192,256]{0,1:T(8,128)(2,1)} fusion(bf16[1024,256]{0,1:T(8,128)(2,1)S(1)} %bitcast.190, bf16[1024,8192]{1,0:T(8,128)(2,1)} %all-gather.2.cloned.1.call-done), kind=kOutput, calls=%fused_computation.19 | convolution fusion | flops 4297064448 | bytes 21495808 | tf_op jit(solution)/shard_map/dot_general | solution.py:43
  507.6 25.8 %convolution_convert_fusion = bf16[8192,1024]{0,1:T(8,128)(2,1)} fusion(bf16[1024,1024]{0,1:T(8,128)(2,1)S(1)} %bitcast.194, bf16[1024,8192]{1,0:T(8,128)(2,1)} %all-gather.2.cloned.1.call-done), kind=kOutput, calls=%fused_computation.10 | convolution fusion | flops 17188257792 | bytes 35651584 | tf_op jit(solution)/shard_map/dot_general | solution.py:43
  533.4 26.4 %pad_maximum_fusion = bf16[8192,1536]{0,1:T(8,128)(2,1)} fusion(bf16[8192,256]{0,1:T(8,128)(2,1)} %convolution_convert_fusion.1, bf16[8192,256]{0,1:T(8,128)(2,1)} %convolution_convert_fusion.2, bf16[8192,1024]{0,1:T(8,128)(2,1)} %convolution_convert_fusion), kind=kLoop, calls=%fused_computation.3 | loop fusion | flops 75497472 | bytes 50331648 | tf_op jit(solution)/shard_map/concatenate | solution.py:158
  565.1 196.7 %reduce-scatter.3.cloned.1.call-done = bf16[256,8192]{1,0:T(8,128)(2,1)} async-done(((bf16[1024,8192]{1,0:T(8,128)(2,1)}), bf16[256,8192]{1,0:T(8,128)(2,1)}) %reduce-scatter.3.cloned.1.call-update) | async-done | bytes 4194320 | tf_op jit(solution)/shard_map/reduce_scatter | solution.py:146
  761.8 5.5 fusion.15
  767.3 41.6 %psum.7 = f32[8192]{0:T(1024)} all-reduce(f32[8192]{0:T(1024)S(1)} %get-tuple-element.24), channel_id=1, replica_groups=mesh['dp'=8,'tp'=4] {'dp','tp'}, use_global_device_ids=true, to_apply=%region_11.12 | all-reduce | flops 8192 | bytes 65536 | tf_op jit(solution)/shard_map/psum | solution.py:156
  808.8 5.9 fusion.11
  814.8 107.3 %reduce-scatter.5.cloned.1.call-done = bf16[1024,1536]{0,1:T(8,128)(2,1)} async-done(((bf16[8192,1536]{0,1:T(8,128)(2,1)}), bf16[1024,1536]{0,1:T(8,128)(2,1)}) %reduce-scatter.5.cloned.1.call-update) | async-done | bytes 3145744 | tf_op jit(solution)/shard_map/reduce_scatter | solution.py:157
  932.5 5.3 copy.105
  (107 shorter events, 58.8 us)
Async XLA Ops:
  7.2 9.2 copy-start.26
  7.2 298.8 %all-gather.2.cloned.1.call-start = ((), (), s32[]{:S(2)}) async-start(), calls=%async_computation.2 | async-start | bytes 20971520 | tf_op jit(solution)/shard_map/all_gather | solution.py:64
  16.3 745.5 %reduce-scatter.3.cloned.1.call-start = ((), (), s32[]{:S(2)}) async-start(), calls=%async_computation.3 | async-start | bytes 20971520 | tf_op jit(solution)/shard_map/reduce_scatter | solution.py:146
  20.1 4.7 copy-start.14
  20.1 4.7 copy-start.16
  305.9 10.3 %copy-start.12 = (bf16[8192,256]{1,0:T(8,128)(2,1)S(1)}, bf16[8192,256]{1,0:T(8,128)(2,1)}, u32[]{:S(2)}) copy-start(bf16[8192,256]{1,0:T(8,128)(2,1)} %param.12) | copy-start | bytes 12582916
  315.4 9.0 copy-start.22
  327.2 23.7 %copy-start.17 = (f32[1024,64]{0,1:T(8,128)S(1)}, f32[1024,64]{0,1:T(8,128)}, u32[]{:S(2)}) copy-start(f32[1024,64]{0,1:T(8,128)} %copy-done.16) | copy-start | bytes 786436
  350.8 2.4 copy-start.3
  361.2 6.9 copy-start.24
  365.9 4.0 copy-start.1
  371.8 4.2 copy-start.9
  386.2 6.9 copy-start.23
  406.3 2.8 copy-start.10
  406.3 2.8 copy-start.21
  406.3 5.1 copy-start.4
  406.3 5.1 copy-start.19
  409.1 5.2 copy-start.2
  413.0 4.3 copy-start.13
  414.3 3.0 copy-start.11
  483.0 439.1 %reduce-scatter.5.cloned.1.call-start = ((), (), s32[]{:S(2)}) async-start(), calls=%async_computation.4 | async-start | bytes 28311552 | tf_op jit(solution)/shard_map/reduce_scatter | solution.py:157
  559.8 202.0 %copy-start.25 = (f32[8192]{0:T(1024)S(1)}, f32[8192]{0:T(1024)}, u32[]{:S(2)}) copy-start(f32[8192]{0:T(1024)} %param.10) | copy-start | bytes 98308
  559.8 202.0 %copy-start.28 = (f32[256]{0:T(256)S(1)}, f32[256]{0:T(256)}, u32[]{:S(2)}) copy-start(f32[256]{0:T(256)} %copy-done.27) | copy-start | bytes 3076
  922.1 8.0 copy-start
  (8 other events, 15.2 us)
Sparse Core Ops, SparseCore 0:
  16.4 289.4 all-gather.1
  483.1 278.6 reduce-scatter.2
  765.4 156.6 reduce-scatter.4
where the time goes:
time: 949 us; the launch traced here: 945 us
  waiting for transfers between devices  584 us (62%)
  matrix products  203 us (21%)
  other arithmetic  68.7 us (7%)
  blocking collectives  41.6 us (4%)
  local copies, waits for them, and re-layouts  32.5 us (3%)
  between operations  14.7 us (2%)
    all_gather x1, waiting for transfers between devices, body(): lax.all_gather((x_hat * norm_gain).astype(jnp.bfloat16), 'tp', axis=0, ti...  280 us
    reduce_scatter x1, waiting for transfers between devices, body(): lax.psum_scatter((total + contract_last(value_flat, w_value)).astype(jnp....  197 us
    reduce_scatter x1, waiting for transfers between devices, body(): lax.psum_scatter(jnp.concatenate([contract_first(normed, query_d), contra...  107 us
    dot_general x3, matrix products, contract_last(): lax.dot_general(left, right, (((1,), (1,)), ((), ())), preferred_element_...  65.4 us
    dot_general x3, matrix products, contract_first(): lax.dot_general(left, right, (((0,), (0,)), ((), ())), preferred_element_...  50.3 us
    psum x1, blocking collectives, body(): gain_grad = lax.psum(jnp.sum(normed_d * x_hat, axis=0), ('dp', 'tp'))  41.6 us
    concatenate x1, other arithmetic, body(): jnp.concatenate([contract_first(normed, query_d), contract_first(normed,...  26.4 us
    dot_general x1, matrix products, body(): jnp.dot(normed, w_query, preferred_element_type=jnp.float32)  23.6 us
  transfers between devices with their start and end apart: 3, of which 3 were waited for; matrix products, arithmetic and copies ran while one was open for 11% of the time, Pallas kernels for 0%

commit v1 on v0

v1 whole, which is shorter than its diff:
```python
import functools

import jax
import jax.numpy as jnp
from jax import lax
from jax.experimental import pallas as pl
from jax.experimental.pallas import tpu as pltpu
from jax.sharding import PartitionSpec as P


HD = 128


epsilon = 1e-05
rope_base = 500000.0


def rope_tables(segment_row, head_dim):
    length = segment_row.shape[0]
    earlier = (segment_row[None, :] < segment_row[:, None]).astype(jnp.int32)
    offset = jnp.arange(length, dtype=jnp.int32) - jnp.sum(earlier, axis=1)
    half_dim = head_dim // 2
    inverse_freq = rope_base ** (-(jnp.arange(half_dim, dtype=jnp.float32) * 2.0 / head_dim))
    angle = offset.astype(jnp.float32)[:, None] * inverse_freq[None, :]
    return (jnp.cos(angle)[:, None, :], jnp.sin(angle)[:, None, :])


def apply_rope(head_rows, cosine_table, sine_table, direction):
    half_dim = head_rows.shape[-1] // 2
    first_half = head_rows[..., :half_dim]
    second_half = head_rows[..., half_dim:]
    return jnp.concatenate(
        [
            first_half * cosine_table - direction * second_half * sine_table,
            second_half * cosine_table + direction * first_half * sine_table,
        ],
        axis=-1,
    )


def contract_first(left, right):
    return lax.dot_general(
        left, right, (((0,), (0,)), ((), ())), preferred_element_type=jnp.float32
    )


def contract_last(left, right):
    return lax.dot_general(
        left, right, (((1,), (1,)), ((), ())), preferred_element_type=jnp.float32
    )


def turn_back(rows_f, cosine, sine):
    return rows_f * cosine + pltpu.roll(rows_f, rows_f.shape[1] // 2, 1) * sine


def attention_kernel(
    block_rows, query_ref, key_ref, value_ref, grad_ref, segment_column, segment_line,
    cosine_ref, sine_ref, attended_ref, query_d_ref, key_d_ref, value_d_ref, key_sum, value_sum,
):
    member = pl.program_id(1)
    seq_len, head_dim = query_ref.shape
    score_scale = float(head_dim) ** (-0.5)

    @pl.when(member == 0)
    def _():
        key_sum[...] = jnp.zeros_like(key_sum)
        value_sum[...] = jnp.zeros_like(value_sum)

    for first in range(0, seq_len, block_rows):
        last = first + block_rows
        query = query_ref[first:last, :]
        grad = grad_ref[first:last, :]
        keys = key_ref[:last, :]
        values = value_ref[:last, :]
        scores = contract_last(query, keys) * score_scale
        row = lax.broadcasted_iota(jnp.int32, scores.shape, 0) + first
        column = lax.broadcasted_iota(jnp.int32, scores.shape, 1)
        same = segment_column[first:last, :] == segment_line[:, :last]
        scores = jnp.where((column <= row) & same, scores, -1e30)
        exponent = jnp.exp(scores - jnp.max(scores, axis=1, keepdims=True))
        probability = exponent * (1.0 / jnp.sum(exponent, axis=1, keepdims=True))
        weights_b = probability.astype(jnp.bfloat16)
        attended = jnp.dot(weights_b, values, preferred_element_type=jnp.float32)
        attended = attended.astype(jnp.bfloat16)
        attended_ref[first:last, :] = attended
        row_delta = jnp.sum(
            grad.astype(jnp.float32) * attended.astype(jnp.float32), axis=1, keepdims=True
        )
        value_sum[:last, :] += contract_first(weights_b, grad)
        prob_d = contract_last(grad, values)
        score_d = (probability * (prob_d - row_delta) * score_scale).astype(jnp.bfloat16)
        query_rot = jnp.dot(score_d, keys, preferred_element_type=jnp.float32)
        query_d_ref[first:last, :] = turn_back(
            query_rot, cosine_ref[first:last, :], sine_ref[first:last, :]
        ).astype(jnp.bfloat16)
        key_sum[:last, :] += contract_first(score_d, query)

    @pl.when(member == pl.num_programs(1) - 1)
    def _():
        key_d_ref[...] = turn_back(key_sum[...], cosine_ref[...], sine_ref[...]).astype(
            jnp.bfloat16
        )
        value_d_ref[...] = value_sum[...].astype(jnp.bfloat16)


def attend(projected, attended_grad, segment_row, cosine_table, sine_table, q_heads, kv_heads):
    seq_len, head_dim = projected.shape[0], HD
    group = q_heads // kv_heads
    block_rows = 256 if seq_len % 256 == 0 else seq_len
    cosine = jnp.concatenate([cosine_table[:, 0], cosine_table[:, 0]], axis=1)
    sine = jnp.concatenate([sine_table[:, 0], -sine_table[:, 0]], axis=1)

    def head(index_of):
        return pl.BlockSpec((seq_len, head_dim), lambda k, m: (0, index_of(k, m)))

    def whole(shape):
        return pl.BlockSpec(shape, lambda k, m: (0, 0))

    of_query = head(lambda k, m: k * group + m)
    of_key = head(lambda k, m: k)
    pairs = q_heads * seq_len * seq_len
    return pl.pallas_call(
        functools.partial(attention_kernel, block_rows),
        grid=(kv_heads, group),
        in_specs=[
            of_query,
            head(lambda k, m: q_heads + k),
            head(lambda k, m: q_heads + kv_heads + k),
            of_query,
            whole((seq_len, 1)),
            whole((1, seq_len)),
            whole((seq_len, head_dim)),
            whole((seq_len, head_dim)),
        ],
        out_specs=[of_query, of_query, of_key, of_key],
        out_shape=[
            jax.ShapeDtypeStruct((seq_len, heads * head_dim), jnp.bfloat16)
            for heads in (q_heads, q_heads, kv_heads, kv_heads)
        ],
        scratch_shapes=[pltpu.VMEM((seq_len, head_dim), jnp.float32)] * 2,
        cost_estimate=pl.CostEstimate(
            flops=8 * pairs * head_dim, bytes_accessed=10 * projected.size, transcendentals=pairs
        ),
    )(
        projected, projected, projected, attended_grad, segment_row[:, None],
        segment_row[None, :], cosine, sine,
    )


def total_over(value, axis):
    size = lax.axis_size(axis)
    if size & (size - 1):
        return lax.psum(value, axis)
    apart = 1
    while apart < size:
        value = value + lax.ppermute(value, axis, [(i, i ^ apart) for i in range(size)])
        apart *= 2
    return value


def right_pairs(low, high):
    return [(i, i + 1) for i in range(low, high)]


def left_pairs(low, high):
    return [(i, i - 1) for i in range(low, high)]


def split_rows(block):
    half = block.shape[0] // 2
    return [block[:half], block[half:]]


def send(pieces, pairs):
    sent = []
    for piece in pieces:
        sent.append(lax.ppermute(piece, "tp", pairs))
    return sent


def end_weights(w_query, w_key, w_value, tp):
    share = w_query.shape[0] // lax.axis_size("dp")
    first = lax.axis_index("dp") * share
    cut = [lax.dynamic_slice_in_dim(w, first, share, 0) for w in (w_query, w_key, w_value)]
    cut = lax.optimization_barrier(jnp.concatenate(cut, axis=1))
    [passed] = send([cut], [(0, 1), (tp - 1, tp - 2)])
    return passed


def shared(passed, after):
    passed, _ = lax.optimization_barrier((passed, after))
    return lax.all_gather(passed, "dp", axis=0, tiled=True)


def line_gather(own, tp, me, steps):
    found = [(own, me)]
    rightward = leftward = own
    for step in range(1, steps):
        rightward = send(rightward, right_pairs(step - 1, tp - 1))
        leftward = send(leftward, left_pairs(1, tp - step + 1))
        if 2 * step >= tp:
            left_over = leftward
            place = jnp.where(me >= step, me - step, me + step)
            if 2 * step > tp:
                empty = (me < step) & (me + step >= tp)
                left_over = [jnp.where(empty, o, l) for o, l in zip(own, leftward)]
                place = jnp.where(empty, me, place)
            chosen = [jnp.where(me >= step, r, l) for r, l in zip(rightward, left_over)]
            found.append((chosen, place))
        else:
            found.append((rightward, (me - step + tp) % tp))
            found.append((leftward, (me + step) % tp))
    return found


def line_scatter(columns_d, weights, far_weights, tp, me, rows):
    def rows_of(place):
        return lax.dynamic_slice(columns_d, (place * rows, 0), (rows, columns_d.shape[1]))

    def part(place):
        return contract_last(rows_of(place), weights)

    def ahead_of(step):
        return jnp.where(me + step < tp, me + step, (me - step + tp) % tp)

    from_left = from_right = None
    first_sent = columns_d
    start = tp - 1
    extra = None
    if far_weights is not None:
        far = lax.optimization_barrier(rows_of(tp - 1 - me))
        far = lax.ppermute(far, "tp", [(0, 1), (tp - 1, tp - 2)])
        start = tp - 2
        own_first = lax.optimization_barrier(part(ahead_of(start)))
        extra = contract_last(far, far_weights)
    for step in range(start, 0, -1):
        if 2 * step >= tp:
            ahead = own_first if extra is not None else part(ahead_of(step))
            if extra is not None:
                ahead, extra = ahead + extra, None
            if from_left is not None:
                ahead = ahead + from_left.astype(jnp.float32) + from_right.astype(jnp.float32)
            rightward = leftward = lax.optimization_barrier(ahead.astype(jnp.bfloat16))
        else:
            rightward = lax.optimization_barrier(part((me + step) % tp))
            leftward = lax.optimization_barrier(part((me - step + tp) % tp))
            if from_left is not None:
                rightward = rightward + from_left.astype(jnp.float32)
                leftward = leftward + from_right.astype(jnp.float32)
            rightward = rightward.astype(jnp.bfloat16)
            leftward = leftward.astype(jnp.bfloat16)
        if step == start:
            first_sent = rightward
        [from_left] = send([rightward], right_pairs(0, tp - step))
        [from_right] = send([leftward], left_pairs(step, tp))
    total = lax.optimization_barrier(part(me))
    if from_left is not None:
        total = total + from_left.astype(jnp.float32) + from_right.astype(jnp.float32)
    return total, first_sent


def body(x_tokens, segment_ids, attended_grad, norm_gain, w_query, w_key, w_value):
    head_dim = HD
    q_heads = w_query.shape[1] // head_dim
    kv_heads = w_key.shape[1] // head_dim
    segment_row = segment_ids[0]
    tp = lax.axis_size("tp")
    me = lax.axis_index("tp")
    rows = x_tokens.shape[0]
    seq_len = tp * rows
    query_cols = w_query.shape[1]
    key_cols = w_key.shape[1]
    relay = tp >= 4
    passed = end_weights(w_query, w_key, w_value, tp) if relay else None
    as_float = x_tokens.astype(jnp.float32)
    inverse = lax.rsqrt(jnp.mean(as_float * as_float, axis=1, keepdims=True) + epsilon)
    x_hat = as_float * inverse
    own = lax.optimization_barrier((x_hat * norm_gain).astype(jnp.bfloat16))
    own = list(lax.optimization_barrier(tuple(split_rows(own))))
    cosine_table, sine_table = rope_tables(segment_row, head_dim)
    weights = lax.optimization_barrier(jnp.concatenate([w_query, w_key, w_value], axis=1))

    def multiply(block, columns):
        return jnp.dot(block, columns, preferred_element_type=jnp.float32)

    def turn(product, place):
        cosine = lax.dynamic_slice_in_dim(cosine_table, place * rows, rows, 0)
        sine = lax.dynamic_slice_in_dim(sine_table, place * rows, rows, 0)
        turned = product[:, : query_cols + key_cols].reshape(rows, -1, head_dim)
        turned = apply_rope(turned, cosine, sine, 1.0).reshape(rows, -1)
        return jnp.concatenate(
            [turned.astype(jnp.bfloat16), product[:, query_cols + key_cols :].astype(jnp.bfloat16)],
            axis=1,
        )

    normed = jnp.zeros((seq_len, x_tokens.shape[1]), jnp.bfloat16)
    projected = jnp.zeros((seq_len, weights.shape[1]), jnp.bfloat16)
    found = line_gather(own, tp, me, tp - 1 if relay else tp)
    far_weights = None
    for index, (pieces, place) in enumerate(found):
        block = lax.optimization_barrier(jnp.concatenate(pieces, axis=0))
        normed = lax.dynamic_update_slice(normed, block, (place * rows, 0))
        source = block
        if relay and index == len(found) - 1:
            inward = [(1, 0), (tp - 2, tp - 1)]
            ready = turn(multiply(block, far_weights), place)
            ready, source = lax.optimization_barrier((ready, block))
            far_product = lax.ppermute(ready, "tp", inward)
        product = multiply(source, weights)
        if relay and index == 0:
            far_weights = shared(passed, product)
        product = turn(product, place)
        projected = lax.dynamic_update_slice(projected, product, (place * rows, 0))
    if relay:
        at_end = (me == 0) | (me == tp - 1)
        far_place = jnp.where(at_end, tp - 1 - me, me)
        kept = lax.dynamic_slice(projected, (far_place * rows, 0), (rows, projected.shape[1]))
        projected = lax.dynamic_update_slice(
            projected, jnp.where(at_end, far_product, kept), (far_place * rows, 0)
        )
        late, _ = lax.optimization_barrier((block, far_product))
        late = lax.ppermute(late, "tp", inward)
        kept = lax.dynamic_slice(normed, (far_place * rows, 0), (rows, normed.shape[1]))
        normed = lax.dynamic_update_slice(
            normed, jnp.where(at_end, late, kept), (far_place * rows, 0)
        )
    attended, query_d, key_d, value_flat = attend(
        projected, attended_grad, segment_row, cosine_table, sine_table, q_heads, kv_heads
    )
    columns_d = lax.optimization_barrier(
        jnp.concatenate([query_d, key_d, value_flat], axis=1)
    )
    normed_d, first_sent = line_scatter(columns_d, weights, far_weights, tp, me, rows)
    held_d, _ = lax.optimization_barrier((columns_d, first_sent))
    weights_d = lax.optimization_barrier(contract_first(normed, held_d).astype(jnp.bfloat16))
    merged = lax.psum_scatter(weights_d, "dp", scatter_dimension=0, tiled=True).astype(jnp.float32)
    gain_part = jnp.sum(weights.astype(jnp.float32) * weights_d.astype(jnp.float32), axis=1)
    gain_part = lax.optimization_barrier(gain_part / norm_gain)
    gain_grad = total_over(total_over(gain_part, "dp"), "tp")
    scaled_d = normed_d * norm_gain
    input_grad = (
        inverse * (scaled_d - x_hat * jnp.mean(scaled_d * x_hat, axis=1, keepdims=True))
    ).astype(jnp.bfloat16)
    grad_query = merged[:, :query_cols]
    grad_key = merged[:, query_cols : query_cols + key_cols]
    grad_value = merged[:, query_cols + key_cols :]
    return (attended, input_grad, gain_grad, grad_query, grad_key, grad_value)


def solution(mesh):
    placed = (
        P(("dp", "tp"), None),
        P("dp", None),
        P("dp", "tp"),
        P(),
        P(None, "tp"),
        P(None, "tp"),
        P(None, "tp"),
    )
    return jax.shard_map(
        body,
        mesh=mesh,
        in_specs=placed,
        out_specs=(
            P("dp", "tp"),
            P(("dp", "tp"), None),
            P(),
            P("dp", "tp"),
            P("dp", "tp"),
            P("dp", "tp"),
        ),
        check_vma=False,
    )
```

time: 949 us -> 739 us (0.78)
  waiting for transfers between devices: 584 us -> 253 us
  starting transfers between devices: 0.12 us -> 72.5 us
  blocking collectives: 41.6 us -> 0 us
  other arithmetic: 68.7 us -> 108 us
  Pallas kernels: 0 us -> 36.9 us
  local copies, waits for them, and re-layouts: 32.5 us -> 63.2 us
  matrix products: 203 us -> 184 us
    reduce_scatter x2 -> x1, waiting for transfers between devices: 304 us -> 0.01 us  [body(): lax.psum_scatter(weights_d, 'dp', scatter_dimension=0, tiled=True)]
    all_gather x1, waiting for transfers between devices: 280 us -> 0.01 us  [shared(): return lax.all_gather(passed, 'dp', axis=0, tiled=True)]
    ppermute x0 -> x21, waiting for transfers between devices: none -> 253 us  [the longest x13 183 us: send(): sent.append(lax.ppermute(piece, 'tp', pairs))]
    ppermute x0 -> x21, starting transfers between devices: none -> 72.4 us  [the longest x13 50.5 us: send(): sent.append(lax.ppermute(piece, 'tp', pairs))]
    psum x1 -> x0, blocking collectives: 41.6 us -> none  [body(): gain_grad = lax.psum(jnp.sum(normed_d * x_hat, axis=0), ('dp', 'tp'))]
    pallas_call x0 -> x1, Pallas kernels: none -> 36.9 us  [attend(): pl.pallas_call(functools.partial(attention_kernel, block_rows), grid=(kv_...]
    reduce_sum x1 -> x2, other arithmetic: 5.5 us -> 29.1 us  [the longest x1 20.5 us: body(): jnp.sum(weights.astype(jnp.float32) * weights_d.astype(jnp.float32), axis=1)]
    sub x2 -> x0, matrix products: 17.9 us -> none  [body(): exponent = jnp.exp(scores - highest)]
  transfers between devices with their start and end apart: 3 -> 23, of which waited for: 3 -> 11; matrix products, arithmetic and copies ran while one was open for 11% -> 38% of each run, Pallas kernels for 0% -> 5%
where the time goes in v1:
time: 739 us; the launch traced here: 733 us
  waiting for transfers between devices  253 us (34%)
  matrix products  184 us (25%)
  other arithmetic  108 us (15%)
  starting transfers between devices  72.5 us (10%)
  local copies, waits for them, and re-layouts  63.2 us (9%)
  Pallas kernels  36.9 us (5%)
  between operations  15.1 us (2%)
    ppermute x13, waiting for transfers between devices, send(): sent.append(lax.ppermute(piece, 'tp', pairs))  183 us
    dot_general x5, matrix products, contract_last(): lax.dot_general(left, right, (((1,), (1,)), ((), ())), preferred_element_...  81.4 us
    dot_general x5, matrix products, multiply(): return jnp.dot(block, columns, preferred_element_type=jnp.float32)  66.3 us
    ppermute x5, waiting for transfers between devices, total_over(): lax.ppermute(value, axis, [(i, i ^ apart) for i in range(size)])  58.1 us
    ppermute x13, starting transfers between devices, send(): sent.append(lax.ppermute(piece, 'tp', pairs))  50.5 us
    pallas_call x1, Pallas kernels, attend(): pl.pallas_call(functools.partial(attention_kernel, block_rows), grid=(kv_...  36.9 us
    dot_general x1, matrix products, contract_first(): lax.dot_general(left, right, (((0,), (0,)), ((), ())), preferred_element_...  36.7 us
    reduce_sum x1, other arithmetic, body(): jnp.sum(weights.astype(jnp.float32) * weights_d.astype(jnp.float32), axis=1)  20.5 us
  transfers between devices with their start and end apart: 23, of which 11 were waited for; matrix products, arithmetic and copies ran while one was open for 38% of the time, Pallas kernels for 5%

profile of v1, /device:TPU:0, one launch (start us, length us, event | category | flops | bytes accessed | tf_op | source)
XLA Modules:
  0.0 733.2 jit_solution(11811897293813366762)
XLA Ops:
  18.7 17.8 %pad_maximum_fusion = bf16[8192,1536]{1,0:T(8,128)(2,1)} fusion(bf16[8192,256]{1,0:T(8,128)(2,1)} %param.13, bf16[8192,256]{1,0:T(8,128)(2,1)} %param.12, bf16[8192,1024]{1,0:T(8,128)(2,1)} %param.11), kind=kLoop, calls=%fused_computation.2 | loop fusion | flops 75497472 | bytes 50331648 | tf_op jit(solution)/shard_map/concatenate | solution.py:282
  42.8 14.2 %fusion.25 = f32[256,1536]{1,0:T(8,128)} fusion(bf16[256,8192]{1,0:T(8,128)(2,1)S(1)} %pad_maximum_fusion.1, bf16[8192,1536]{1,0:T(8,128)(2,1)} %pad_maximum_fusion), kind=kOutput, calls=%fused_computation.94 | convolution fusion | flops 6442450944 | bytes 30932992 | tf_op jit(solution)/shard_map/dot_general | solution.py:285
  57.0 27.7 %collective-permute-done.8 = bf16[1024,1536]{1,0:T(8,128)(2,1)} collective-permute-done((bf16[1024,1536]{1,0:T(8,128)(2,1)}, bf16[1024,1536]{1,0:T(8,128)(2,1)}, u32[]{:S(2)}, u32[]{:S(2)}) %collective-permute-start.8) | collective-permute-done | bytes 3145760 | tf_op jit(solution)/shard_map/ppermute | solution.py:178
  140.4 39.9 %collective-permute-done.1 = bf16[128,8192]{1,0:T(8,128)(2,1)} collective-permute-done((bf16[128,8192]{1,0:T(8,128)(2,1)S(1)}, bf16[128,8192]{1,0:T(8,128)(2,1)}, u32[]{:S(2)}, u32[]{:S(2)}) %collective-permute-start.1) | collective-permute-done | bytes 2097184 | tf_op jit(solution)/shard_map/ppermute | solution.py:178
  182.7 13.2 %fusion.26 = f32[256,1536]{1,0:T(8,128)S(1)} fusion(bf16[256,8192]{1,0:T(8,128)(2,1)S(1)} %pad_maximum_fusion.2, bf16[8192,1536]{1,0:T(8,128)(2,1)} %pad_maximum_fusion), kind=kOutput, calls=%fused_computation.95 | convolution fusion | flops 6442450944 | bytes 30932992 | tf_op jit(solution)/shard_map/dot_general | solution.py:285
  199.3 13.2 %fusion.27 = f32[256,1536]{1,0:T(8,128)S(1)} fusion(bf16[256,8192]{1,0:T(8,128)(2,1)S(1)} %pad_maximum_fusion.3, bf16[8192,1536]{1,0:T(8,128)(2,1)} %pad_maximum_fusion), kind=kOutput, calls=%fused_computation.96 | convolution fusion | flops 6442450944 | bytes 30932992 | tf_op jit(solution)/shard_map/dot_general | solution.py:285
  231.9 38.8 %collective-permute-done.5 = bf16[128,8192]{1,0:T(8,128)(2,1)S(1)} collective-permute-done((bf16[128,8192]{1,0:T(8,128)(2,1)}, bf16[128,8192]{1,0:T(8,128)(2,1)S(1)}, u32[]{:S(2)}, u32[]{:S(2)}) %collective-permute-start.5) | collective-permute-done | bytes 2097184 | tf_op jit(solution)/shard_map/ppermute | solution.py:178
  271.0 41.4 %collective-permute-done.7 = bf16[128,8192]{1,0:T(8,128)(2,1)S(1)} collective-permute-done((bf16[128,8192]{1,0:T(8,128)(2,1)}, bf16[128,8192]{1,0:T(8,128)(2,1)S(1)}, u32[]{:S(2)}, u32[]{:S(2)}) %collective-permute-start.7) | collective-permute-done | bytes 2097184 | tf_op jit(solution)/shard_map/ppermute | solution.py:178
  317.5 12.8 %fusion.28 = f32[256,1536]{1,0:T(8,128)S(1)} fusion(bf16[256,8192]{1,0:T(8,128)(2,1)} %copy-done.5, bf16[8192,1536]{1,0:T(8,128)(2,1)} %all-gather.2.cloned.1.call-done), kind=kOutput, calls=%fused_computation.97 | convolution fusion | flops 6442450944 | bytes 30932992 | tf_op jit(solution)/shard_map/dot_general | solution.py:285
  333.7 12.8 %fusion.29 = f32[256,1536]{1,0:T(8,128)S(1)} fusion(bf16[256,8192]{1,0:T(8,128)(2,1)} %copy-done.5, bf16[8192,1536]{1,0:T(8,128)(2,1)} %pad_maximum_fusion), kind=kOutput, calls=%fused_computation.98 | convolution fusion | flops 6442450944 | bytes 30932992 | tf_op jit(solution)/shard_map/dot_general | solution.py:285
  354.7 36.9 %shard_map.118 = (bf16[1024,1024]{1,0:T(8,128)(2,1)}, bf16[1024,1024]{1,0:T(8,128)(2,1)}, bf16[1024,256]{1,0:T(8,128)(2,1)}, bf16[1024,256]{1,0:T(8,128)(2,1)}) custom-call(bf16[1024,1536]{1,0:T(8,128)(2,1)} %select_dynamic-update-slice_fusion.1.query_ref.key_ref.value_ref, bf16[1024,1536]{1,0:T(8,128)(2,1)} %select_dynamic-update-slice_fusion.1.query_ref.key_ref.value_ref, ...), custom_call_target="tpu_custom_call" | custom-call | flops 8589934592 | bytes 15728640 | tf_op jit(solution)/shard_map/pallas_call | solution.py:123
  401.9 13.6 %fusion.12 = f32[256,8192]{1,0:T(8,128)} fusion(bf16[8192,1536]{1,0:T(8,128)(2,1)} %pad_maximum_fusion, bf16[1024,1536]{1,0:T(8,128)(2,1)S(1)} %pad_maximum_fusion.6, s32[]{:T(128)S(6)} %select_n.119), kind=kOutput, calls=%fused_computation.36 | convolution fusion | flops 6442450944 | bytes 34340868 | tf_op jit(solution)/shard_map/dot_general | solution.py:48
  415.4 15.4 %fusion.3 = bf16[256,8192]{1,0:T(8,128)(2,1)} fusion(f32[256,8192]{1,0:T(8,128)} %fusion.12, bf16[256,1536]{1,0:T(8,128)(2,1)} %collective-permute-done.10, bf16[8192,1536]{1,0:T(8,128)(2,1)} %all-gather.2.cloned.1.call-done), kind=kOutput, calls=%fused_computation.9 | convolution fusion | flops 6446645248 | bytes 38535168 | tf_op jit(solution)/shard_map/dot_general | solution.py:48
  430.9 11.2 %collective-permute-done.15 = bf16[256,8192]{1,0:T(8,128)(2,1)} collective-permute-done((bf16[256,8192]{1,0:T(8,128)(2,1)}, bf16[256,8192]{1,0:T(8,128)(2,1)}, u32[]{:S(2)}, u32[]{:S(2)}) %collective-permute-start.15) | collective-permute-done | bytes 4194336 | tf_op jit(solution)/shard_map/ppermute | solution.py:323
  449.1 36.7 %convolution_convert_fusion = bf16[8192,1536]{1,0:T(8,128)(2,1)} fusion(bf16[1024,8192]{1,0:T(8,128)(2,1)} %select_dynamic-update-slice_fusion, bf16[1024,1536]{1,0:T(8,128)(2,1)S(1)} %pad_maximum_fusion.6), kind=kOutput, calls=%fused_computation.1 | convolution fusion | flops 25782386688 | bytes 45088768 | tf_op jit(solution)/shard_map/dot_general | solution.py:42
  492.0 18.3 %fusion.10 = f32[256,8192]{1,0:T(8,128)} fusion(bf16[8192,1536]{1,0:T(8,128)(2,1)} %pad_maximum_fusion, bf16[1024,1536]{1,0:T(8,128)(2,1)S(1)} %pad_maximum_fusion.6, s32[]{:T(128)S(6)} %select_n.104), kind=kOutput, calls=%fused_computation.34 | convolution fusion | flops 6442450944 | bytes 34340868 | tf_op jit(solution)/shard_map/dot_general | solution.py:48
  510.4 20.6 %fusion.14 = f32[256,8192]{1,0:T(8,128)} fusion(bf16[8192,1536]{1,0:T(8,128)(2,1)} %pad_maximum_fusion, bf16[1024,1536]{1,0:T(8,128)(2,1)S(1)} %pad_maximum_fusion.6, s32[]{:T(128)S(6)} %select_n.106), kind=kOutput, calls=%fused_computation.38 | convolution fusion | flops 6442450944 | bytes 34340868 | tf_op jit(solution)/shard_map/dot_general | solution.py:48
  531.0 8.9 %add_convert_fusion = bf16[256,8192]{1,0:T(8,128)(2,1)} fusion(f32[256,8192]{1,0:T(8,128)} %fusion.10, bf16[256,8192]{1,0:T(8,128)(2,1)} %collective-permute-done.13), kind=kLoop, calls=%fused_computation.17 | loop fusion | flops 6291456 | bytes 16777216 | tf_op jit(solution)/shard_map/convert_element_type | solution.py:252
  541.1 35.0 %collective-permute-done.11 = bf16[256,8192]{1,0:T(8,128)(2,1)} collective-permute-done((bf16[256,8192]{1,0:T(8,128)(2,1)}, bf16[256,8192]{1,0:T(8,128)(2,1)}, u32[]{:S(2)}, u32[]{:S(2)}) %collective-permute-start.11) | collective-permute-done | bytes 4194336 | tf_op jit(solution)/shard_map/ppermute | solution.py:178
  581.4 16.8 %collective-permute-start.12 = (bf16[256,8192]{1,0:T(8,128)(2,1)}, bf16[256,8192]{1,0:T(8,128)(2,1)}, u32[]{:S(2)}, u32[]{:S(2)}) collective-permute-start(bf16[256,8192]{1,0:T(8,128)(2,1)} %add_convert_fusion.1), channel_id=1, source_target_pairs={{0,1},{1,2},{2,3},{4,5},{5,6},{6,7},{8,9},{9,10},{10,11},{12,13},{... | collective-permute-start | bytes 12582920 | tf_op jit(solution)/shard_map/ppermute | solution.py:178
  598.2 20.5 %multiply_reduce_fusion = f32[8192]{0:T(1024)S(1)} fusion(bf16[8192,1536]{1,0:T(8,128)(2,1)} %convolution_convert_fusion, bf16[8192,1536]{1,0:T(8,128)(2,1)} %pad_maximum_fusion), kind=kLoop, calls=%fused_computation | loop fusion | flops 50323456 | bytes 50364416 | tf_op jit(solution)/shard_map/reduce_sum | solution.py:338
  630.7 51.3 %collective-permute-done.19 = f32[8192]{0:T(1024)S(1)} collective-permute-done((f32[8192]{0:T(1024)S(1)}, f32[8192]{0:T(1024)S(1)}, u32[]{:S(2)}, u32[]{:S(2)}) %collective-permute-start.19) | collective-permute-done | bytes 32800 | tf_op jit(solution)/shard_map/ppermute | solution.py:157
  688.9 13.5 %fusion.16 = f32[256,8192]{1,0:T(8,128)} fusion(bf16[8192,1536]{1,0:T(8,128)(2,1)} %pad_maximum_fusion, bf16[1024,1536]{1,0:T(8,128)(2,1)S(1)} %pad_maximum_fusion.6, s32[]{:T(128)S(6)} %select_n.102), kind=kOutput, calls=%fused_computation.40 | convolution fusion | flops 6442450944 | bytes 34340868 | tf_op jit(solution)/shard_map/dot_general | solution.py:48
  703.1 8.5 %fusion.5 = f32[256]{0:T(256)S(1)} fusion(bf16[256,8192]{1,0:T(8,128)(2,1)} %param.7, f32[256]{0:T(256)S(1)} %copy-done.28, f32[8192]{0:T(1024)S(1)} %copy-done.18, bf16[256,8192]{1,0:T(8,128)(2,1)} %collective-permute-done.14, f32[256,8192]{1,0:T(8,128)} %fusion.16, bf16[256,8192]{1,0:T(8,128)(2,1)} %collective-permute-done.12), kind=kLoop, calls=%fused_computation.11 | loop fusion | flops 18874112 | bytes 21006336 | tf_op jit(solution)/shard_map/reduce_sum | solution.py:343
  (183 shorter events, 178.9 us)
Async XLA Ops:
  7.2 310.3 %all-gather.2.cloned.1.call-start = ((), (), s32[]{:S(2)}) async-start(), calls=%async_computation.1 | async-start | bytes 28311552 | tf_op jit(solution)/shard_map/all_gather | solution.py:193
  12.1 72.6 %collective-permute-start.8 = (bf16[1024,1536]{1,0:T(8,128)(2,1)}, bf16[1024,1536]{1,0:T(8,128)(2,1)}, u32[]{:S(2)}, u32[]{:S(2)}) collective-permute-start(bf16[1024,1536]{1,0:T(8,128)(2,1)} %pad_maximum_fusion.5), channel_id=1, source_target_pairs={{0,1},{3,2},{4,5},{7,6},{8,9},{11,10},{12,13},{15,14},{16,17},{19,... | collective-permute-start | bytes 9437192 | tf_op jit(solution)/shard_map/ppermute | solution.py:178
  84.7 635.8 %reduce-scatter.2.cloned.1.call-start = ((), (), s32[]{:S(2)}) async-start(), calls=%async_computation.2 | async-start | bytes 28311552 | tf_op jit(solution)/shard_map/reduce_scatter | solution.py:337
  84.7 112.0 %collective-permute-start.2 = (bf16[128,8192]{1,0:T(8,128)(2,1)}, bf16[128,8192]{1,0:T(8,128)(2,1)}, u32[]{:S(2)}, u32[]{:S(2)}) collective-permute-start(bf16[128,8192]{1,0:T(8,128)(2,1)} %copy-done.11), channel_id=1, source_target_pairs={{1,0},{2,1},{3,2},{5,4},{6,5},{7,6},{9,8},{10,9},{11,10},{13,12},{... | collective-permute-start | bytes 6291464 | tf_op jit(solution)/shard_map/ppermute | solution.py:178
  86.0 54.3 %collective-permute-start = (bf16[128,8192]{1,0:T(8,128)(2,1)}, bf16[128,8192]{1,0:T(8,128)(2,1)}, u32[]{:S(2)}, u32[]{:S(2)}) collective-permute-start(bf16[128,8192]{1,0:T(8,128)(2,1)} %copy-done.11), channel_id=1, source_target_pairs={{0,1},{1,2},{2,3},{4,5},{5,6},{6,7},{8,9},{9,10},{10,11},{12,13},{... | collective-permute-start | bytes 6291464 | tf_op jit(solution)/shard_map/ppermute | solution.py:178
  92.4 104.4 %collective-permute-start.3 = (bf16[128,8192]{1,0:T(8,128)(2,1)S(1)}, bf16[128,8192]{1,0:T(8,128)(2,1)}, u32[]{:S(2)}, u32[]{:S(2)}) collective-permute-start(bf16[128,8192]{1,0:T(8,128)(2,1)S(1)} %get-tuple-element.18), channel_id=1, source_target_pairs={{1,0},{2,1},{3,2},{5,4},{6,5},{7,6},{9,8},{10,9},{11,10},{13,12},{... | collective-permute-start | bytes 6291464 | tf_op jit(solution)/shard_map/ppermute | solution.py:178
  93.7 86.6 %collective-permute-start.1 = (bf16[128,8192]{1,0:T(8,128)(2,1)S(1)}, bf16[128,8192]{1,0:T(8,128)(2,1)}, u32[]{:S(2)}, u32[]{:S(2)}) collective-permute-start(bf16[128,8192]{1,0:T(8,128)(2,1)S(1)} %get-tuple-element.18), channel_id=1, source_target_pairs={{0,1},{1,2},{2,3},{4,5},{5,6},{6,7},{8,9},{9,10},{10,11},{12,13},{... | collective-permute-start | bytes 6291464 | tf_op jit(solution)/shard_map/ppermute | solution.py:178
  218.3 52.4 %collective-permute-start.5 = (bf16[128,8192]{1,0:T(8,128)(2,1)}, bf16[128,8192]{1,0:T(8,128)(2,1)S(1)}, u32[]{:S(2)}, u32[]{:S(2)}) collective-permute-start(bf16[128,8192]{1,0:T(8,128)(2,1)} %collective-permute-done.2), channel_id=1, source_target_pairs={{1,0},{2,1},{5,4},{6,5},{9,8},{10,9},{13,12},{14,13},{17,16},{18,1... | collective-permute-start | bytes 6291464 | tf_op jit(solution)/shard_map/ppermute | solution.py:178
  220.1 50.6 %collective-permute-start.4 = (bf16[128,8192]{1,0:T(8,128)(2,1)}, bf16[128,8192]{1,0:T(8,128)(2,1)S(1)}, u32[]{:S(2)}, u32[]{:S(2)}) collective-permute-start(bf16[128,8192]{1,0:T(8,128)(2,1)} %collective-permute-done), channel_id=1, source_target_pairs={{1,2},{2,3},{5,6},{6,7},{9,10},{10,11},{13,14},{14,15},{17,18},{18... | collective-permute-start | bytes 6291464 | tf_op jit(solution)/shard_map/ppermute | solution.py:178
  220.9 91.5 %collective-permute-start.7 = (bf16[128,8192]{1,0:T(8,128)(2,1)}, bf16[128,8192]{1,0:T(8,128)(2,1)S(1)}, u32[]{:S(2)}, u32[]{:S(2)}) collective-permute-start(bf16[128,8192]{1,0:T(8,128)(2,1)} %collective-permute-done.3), channel_id=1, source_target_pairs={{1,0},{2,1},{5,4},{6,5},{9,8},{10,9},{13,12},{14,13},{17,16},{18,1... | collective-permute-start | bytes 6291464 | tf_op jit(solution)/shard_map/ppermute | solution.py:178
  222.2 90.2 %collective-permute-start.6 = (bf16[128,8192]{1,0:T(8,128)(2,1)}, bf16[128,8192]{1,0:T(8,128)(2,1)S(1)}, u32[]{:S(2)}, u32[]{:S(2)}) collective-permute-start(bf16[128,8192]{1,0:T(8,128)(2,1)} %collective-permute-done.1), channel_id=1, source_target_pairs={{1,2},{2,3},{5,6},{6,7},{9,10},{10,11},{13,14},{14,15},{17,18},{18... | collective-permute-start | bytes 6291464 | tf_op jit(solution)/shard_map/ppermute | solution.py:178
  332.4 18.4 %collective-permute-start.9 = (bf16[256,1536]{1,0:T(8,128)(2,1)S(1)}, bf16[256,1536]{1,0:T(8,128)(2,1)}, u32[]{:S(2)}, u32[]{:S(2)}) collective-permute-start(bf16[256,1536]{1,0:T(8,128)(2,1)S(1)} %pad_maximum_fusion.7), channel_id=1, source_target_pairs={{1,0},{2,3},{5,4},{6,7},{9,8},{10,11},{13,12},{14,15},{17,16},{18,... | collective-permute-start | bytes 2359304 | tf_op jit(solution)/shard_map/ppermute | solution.py:309
  350.8 91.2 %collective-permute-start.15 = (bf16[256,8192]{1,0:T(8,128)(2,1)}, bf16[256,8192]{1,0:T(8,128)(2,1)}, u32[]{:S(2)}, u32[]{:S(2)}) collective-permute-start(bf16[256,8192]{1,0:T(8,128)(2,1)} %copy-done.5), channel_id=1, source_target_pairs={{1,0},{2,3},{5,4},{6,7},{9,8},{10,11},{13,12},{14,15},{17,16},{18,... | collective-permute-start | bytes 12582920 | tf_op jit(solution)/shard_map/ppermute | solution.py:323
  394.6 20.9 %collective-permute-start.10 = (bf16[256,1536]{1,0:T(8,128)(2,1)}, bf16[256,1536]{1,0:T(8,128)(2,1)}, u32[]{:S(2)}, u32[]{:S(2)}) collective-permute-start(bf16[256,1536]{1,0:T(8,128)(2,1)} %constant_dynamic-slice_fusion), channel_id=1, source_target_pairs={{0,1},{3,2},{4,5},{7,6},{8,9},{11,10},{12,13},{15,14},{16,17},{19,... | collective-permute-start | bytes 2359304 | tf_op jit(solution)/shard_map/ppermute | solution.py:233
  485.9 45.1 %collective-permute-start.13 = (bf16[256,8192]{1,0:T(8,128)(2,1)}, bf16[256,8192]{1,0:T(8,128)(2,1)}, u32[]{:S(2)}, u32[]{:S(2)}) collective-permute-start(bf16[256,8192]{1,0:T(8,128)(2,1)} %fusion.3), channel_id=1, source_target_pairs={{2,1},{3,2},{6,5},{7,6},{10,9},{11,10},{14,13},{15,14},{18,17},{19... | collective-permute-start | bytes 12582920 | tf_op jit(solution)/shard_map/ppermute | solution.py:178
  488.6 87.5 %collective-permute-start.11 = (bf16[256,8192]{1,0:T(8,128)(2,1)}, bf16[256,8192]{1,0:T(8,128)(2,1)}, u32[]{:S(2)}, u32[]{:S(2)}) collective-permute-start(bf16[256,8192]{1,0:T(8,128)(2,1)} %fusion.3), channel_id=1, source_target_pairs={{0,1},{1,2},{4,5},{5,6},{8,9},{9,10},{12,13},{13,14},{16,17},{17,1... | collective-permute-start | bytes 12582920 | tf_op jit(solution)/shard_map/ppermute | solution.py:178
  531.0 45.1 %copy-start.10 = (f32[256,8192]{1,0:T(8,128)S(1)}, f32[256,8192]{1,0:T(8,128)}, u32[]{:S(2)}) copy-start(f32[256,8192]{1,0:T(8,128)} %fusion.14) | copy-start | bytes 25165828
  539.8 163.2 %collective-permute-start.14 = (bf16[256,8192]{1,0:T(8,128)(2,1)}, bf16[256,8192]{1,0:T(8,128)(2,1)}, u32[]{:S(2)}, u32[]{:S(2)}) collective-permute-start(bf16[256,8192]{1,0:T(8,128)(2,1)} %add_convert_fusion), channel_id=1, source_target_pairs={{1,0},{2,1},{3,2},{5,4},{6,5},{7,6},{9,8},{10,9},{11,10},{13,12},{... | collective-permute-start | bytes 12582920 | tf_op jit(solution)/shard_map/ppermute | solution.py:178
  581.4 121.6 %collective-permute-start.12 = (bf16[256,8192]{1,0:T(8,128)(2,1)}, bf16[256,8192]{1,0:T(8,128)(2,1)}, u32[]{:S(2)}, u32[]{:S(2)}) collective-permute-start(bf16[256,8192]{1,0:T(8,128)(2,1)} %add_convert_fusion.1), channel_id=1, source_target_pairs={{0,1},{1,2},{2,3},{4,5},{5,6},{6,7},{8,9},{9,10},{10,11},{12,13},{... | collective-permute-start | bytes 12582920 | tf_op jit(solution)/shard_map/ppermute | solution.py:178
  618.8 1.3 collective-permute-start.16
  620.1 4.7 collective-permute-start.17
  624.8 4.7 collective-permute-start.18
  629.5 52.5 %collective-permute-start.19 = (f32[8192]{0:T(1024)S(1)}, f32[8192]{0:T(1024)S(1)}, u32[]{:S(2)}, u32[]{:S(2)}) collective-permute-start(f32[8192]{0:T(1024)S(1)} %add.164), channel_id=1, source_target_pairs={{0,1},{1,0},{2,3},{3,2},{4,5},{5,4},{6,7},{7,6},{8,9},{9,8},{10,11... | collective-permute-start | bytes 98312 | tf_op jit(solution)/shard_map/ppermute | solution.py:157
  682.0 20.4 %collective-permute-start.20 = (f32[8192]{0:T(1024)S(1)}, f32[8192]{0:T(1024)S(1)}, u32[]{:S(2)}, u32[]{:S(2)}) collective-permute-start(f32[8192]{0:T(1024)S(1)} %add.165), channel_id=1, source_target_pairs={{0,2},{1,3},{2,0},{3,1},{4,6},{5,7},{6,4},{7,5},{8,10},{9,11},{10,... | collective-permute-start | bytes 98312 | tf_op jit(solution)/shard_map/ppermute | solution.py:157
  (29 other events, 262.9 us)
Sparse Core Ops, SparseCore 0:
  84.8 126.3 all-gather.1
  486.0 161.6 reduce-scatter.1

commit v2 on v1

--- a/solution.py
+++ b/solution.py
@@ -194,7 +194,7 @@
 
 
 def line_gather(own, tp, me, steps):
-    found = [(own, me)]
+    found = [[(own, me)]]
     rightward = leftward = own
     for step in range(1, steps):
         rightward = send(rightward, right_pairs(step - 1, tp - 1))
@@ -207,57 +207,77 @@
                 left_over = [jnp.where(empty, o, l) for o, l in zip(own, leftward)]
                 place = jnp.where(empty, me, place)
             chosen = [jnp.where(me >= step, r, l) for r, l in zip(rightward, left_over)]
-            found.append((chosen, place))
+            found.append([(chosen, place)])
         else:
-            found.append((rightward, (me - step + tp) % tp))
-            found.append((leftward, (me + step) % tp))
+            before, after = (me - step + tp) % tp, (me + step) % tp
+            found.append([(rightward, before), (leftward, after)])
     return found
 
 
-def line_scatter(columns_d, weights, far_weights, tp, me, rows):
+def line_scatter(columns_d, weights, far_weights, tp, me, rows, between):
+    features = weights.shape[0]
+    halves = ((0, features // 2), (features // 2, features))
+
     def rows_of(place):
         return lax.dynamic_slice(columns_d, (place * rows, 0), (rows, columns_d.shape[1]))
 
     def part(place):
-        return contract_last(rows_of(place), weights)
+        return lax.optimization_barrier(contract_last(rows_of(place), weights))
 
     def ahead_of(step):
         return jnp.where(me + step < tp, me + step, (me - step + tp) % tp)
 
-    from_left = from_right = None
-    first_sent = columns_d
+    def plus(sums, index, received):
+        low, high = halves[index]
+        sums = sums[:, low:high]
+        for item in received:
+            sums = sums + item.astype(jnp.float32)
+        return sums
+
+    far = None
     start = tp - 1
-    extra = None
     if far_weights is not None:
         far = lax.optimization_barrier(rows_of(tp - 1 - me))
         far = lax.ppermute(far, "tp", [(0, 1), (tp - 1, tp - 2)])
         start = tp - 2
-        own_first = lax.optimization_barrier(part(ahead_of(start)))
-        extra = contract_last(far, far_weights)
+    result = None
+    received = [(), ()]
     for step in range(start, 0, -1):
-        if 2 * step >= tp:
-            ahead = own_first if extra is not None else part(ahead_of(step))
-            if extra is not None:
-                ahead, extra = ahead + extra, None
-            if from_left is not None:
-                ahead = ahead + from_left.astype(jnp.float32) + from_right.astype(jnp.float32)
-            rightward = leftward = lax.optimization_barrier(ahead.astype(jnp.bfloat16))
+        joint = 2 * step >= tp
+        if joint:
+            right_part = left_part = part(ahead_of(step))
         else:
-            rightward = lax.optimization_barrier(part((me + step) % tp))
-            leftward = lax.optimization_barrier(part((me - step + tp) % tp))
-            if from_left is not None:
-                rightward = rightward + from_left.astype(jnp.float32)
-                leftward = leftward + from_right.astype(jnp.float32)
-            rightward = rightward.astype(jnp.bfloat16)
-            leftward = leftward.astype(jnp.bfloat16)
-        if step == start:
-            first_sent = rightward
-        [from_left] = send([rightward], right_pairs(0, tp - step))
-        [from_right] = send([leftward], left_pairs(step, tp))
-    total = lax.optimization_barrier(part(me))
-    if from_left is not None:
-        total = total + from_left.astype(jnp.float32) + from_right.astype(jnp.float32)
-    return total, first_sent
+            both = [rows_of((me + step) % tp), rows_of((me - step + tp) % tp)]
+            both = contract_last(jnp.concatenate(both, axis=0), weights)
+            both = lax.optimization_barrier(both)
+            right_part, left_part = both[:rows], both[rows:]
+        sent = []
+        for index, (low, high) in enumerate(halves):
+            got = received[index]
+            if step == start and far is not None:
+                got = (contract_last(far, far_weights[low:high]),)
+            if joint:
+                rightward = leftward = lax.optimization_barrier(
+                    plus(right_part, index, got).astype(jnp.bfloat16)
+                )
+            else:
+                rightward = plus(right_part, index, got[:1]).astype(jnp.bfloat16)
+                leftward = plus(left_part, index, got[1:]).astype(jnp.bfloat16)
+                both, rightward, leftward = lax.optimization_barrier((both, rightward, leftward))
+                right_part, left_part = both[:rows], both[rows:]
+            [from_left] = send([rightward], right_pairs(0, tp - step))
+            [from_right] = send([leftward], left_pairs(step, tp))
+            sent.append((from_left, from_right))
+            if result is None:
+                result = between(rightward)
+                if far is not None:
+                    far, _ = lax.optimization_barrier((far, result))
+        received = sent
+    if result is None:
+        result = between(columns_d)
+    total = part(me)
+    total = [plus(total, index, received[index]) for index in range(2)]
+    return jnp.concatenate(total, axis=1), result
 
 
 def body(x_tokens, segment_ids, attended_grad, norm_gain, w_query, w_key, w_value):
@@ -298,20 +318,23 @@
     projected = jnp.zeros((seq_len, weights.shape[1]), jnp.bfloat16)
     found = line_gather(own, tp, me, tp - 1 if relay else tp)
     far_weights = None
-    for index, (pieces, place) in enumerate(found):
-        block = lax.optimization_barrier(jnp.concatenate(pieces, axis=0))
-        normed = lax.dynamic_update_slice(normed, block, (place * rows, 0))
+    for index, batch in enumerate(found):
+        block = jnp.concatenate([piece for pieces, _ in batch for piece in pieces], axis=0)
+        block = lax.optimization_barrier(block)
         source = block
         if relay and index == len(found) - 1:
             inward = [(1, 0), (tp - 2, tp - 1)]
-            ready = turn(multiply(block, far_weights), place)
+            ready = turn(multiply(block, far_weights), batch[0][1])
             ready, source = lax.optimization_barrier((ready, block))
             far_product = lax.ppermute(ready, "tp", inward)
         product = multiply(source, weights)
         if relay and index == 0:
             far_weights = shared(passed, product)
-        product = turn(product, place)
-        projected = lax.dynamic_update_slice(projected, product, (place * rows, 0))
+        for number, (_, place) in enumerate(batch):
+            mine = slice(number * rows, (number + 1) * rows)
+            normed = lax.dynamic_update_slice(normed, block[mine], (place * rows, 0))
+            turned = turn(product[mine], place)
+            projected = lax.dynamic_update_slice(projected, turned, (place * rows, 0))
     if relay:
         at_end = (me == 0) | (me == tp - 1)
         far_place = jnp.where(at_end, tp - 1 - me, me)
@@ -319,8 +342,10 @@
         projected = lax.dynamic_update_slice(
             projected, jnp.where(at_end, far_product, kept), (far_place * rows, 0)
         )
-        late, _ = lax.optimization_barrier((block, far_product))
-        late = lax.ppermute(late, "tp", inward)
+        early = rows // 4
+        late, _ = lax.optimization_barrier((block[early:], far_product))
+        late = send([lax.optimization_barrier(block[:early])], inward) + send([late], inward)
+        late = jnp.concatenate(late, axis=0)
         kept = lax.dynamic_slice(normed, (far_place * rows, 0), (rows, normed.shape[1]))
         normed = lax.dynamic_update_slice(
             normed, jnp.where(at_end, late, kept), (far_place * rows, 0)
@@ -331,9 +356,14 @@
     columns_d = lax.optimization_barrier(
         jnp.concatenate([query_d, key_d, value_flat], axis=1)
     )
-    normed_d, first_sent = line_scatter(columns_d, weights, far_weights, tp, me, rows)
-    held_d, _ = lax.optimization_barrier((columns_d, first_sent))
-    weights_d = lax.optimization_barrier(contract_first(normed, held_d).astype(jnp.bfloat16))
+
+    def weights_grad(after):
+        held_d, _ = lax.optimization_barrier((columns_d, after))
+        return lax.optimization_barrier(contract_first(normed, held_d).astype(jnp.bfloat16))
+
+    normed_d, weights_d = line_scatter(
+        columns_d, weights, far_weights, tp, me, rows, weights_grad
+    )
     merged = lax.psum_scatter(weights_d, "dp", scatter_dimension=0, tiled=True).astype(jnp.float32)
     gain_part = jnp.sum(weights.astype(jnp.float32) * weights_d.astype(jnp.float32), axis=1)
     gain_part = lax.optimization_barrier(gain_part / norm_gain)

time: 739 us -> 707 us (0.957)
  waiting for transfers between devices: 253 us -> 229 us
  matrix products: 184 us -> 173 us
    ppermute x5, waiting for transfers between devices: 58.1 us -> 43.3 us  [total_over(): lax.ppermute(value, axis, [(i, i ^ apart) for i in range(size)])]
    ppermute x1 -> x0, waiting for transfers between devices: 11.2 us -> none  [body(): late = lax.ppermute(late, 'tp', inward)]
    add x0 -> x1, other arithmetic: none -> 11.1 us  [plus(): sums = sums + item.astype(jnp.float32)]
    dot_general x5 -> x4, matrix products: 66.3 us -> 60.8 us  [multiply(): return jnp.dot(block, columns, preferred_element_type=jnp.float32)]
    ppermute x13 -> x19, starting transfers between devices: 50.5 us -> 55.8 us  [send(): sent.append(lax.ppermute(piece, 'tp', pairs))]
    ppermute x13 -> x19, waiting for transfers between devices: 183 us -> 181 us  [send(): sent.append(lax.ppermute(piece, 'tp', pairs))]
  transfers between devices with their start and end apart: 23 -> 28, of which waited for: 11 -> 13; matrix products, arithmetic and copies ran while one was open for 38% -> 41% of each run, Pallas kernels for 5% -> 5%
where the time goes in v2:
time: 707 us; the launch traced here: 701 us
  waiting for transfers between devices  229 us (32%)
  matrix products  173 us (24%)
  other arithmetic  109 us (15%)
  starting transfers between devices  72.7 us (10%)
  local copies, waits for them, and re-layouts  65.6 us (9%)
  Pallas kernels  36.9 us (5%)
  between operations  15 us (2%)
    ppermute x19, waiting for transfers between devices, send(): sent.append(lax.ppermute(piece, 'tp', pairs))  181 us
    dot_general x5, matrix products, contract_last(): lax.dot_general(left, right, (((1,), (1,)), ((), ())), preferred_element_...  75.2 us
    dot_general x4, matrix products, multiply(): return jnp.dot(block, columns, preferred_element_type=jnp.float32)  60.8 us
    ppermute x19, starting transfers between devices, send(): sent.append(lax.ppermute(piece, 'tp', pairs))  55.8 us
    ppermute x5, waiting for transfers between devices, total_over(): lax.ppermute(value, axis, [(i, i ^ apart) for i in range(size)])  43.3 us
    pallas_call x1, Pallas kernels, attend(): pl.pallas_call(functools.partial(attention_kernel, block_rows), grid=(kv_...  36.9 us
    dot_general x1, matrix products, contract_first(): lax.dot_general(left, right, (((0,), (0,)), ((), ())), preferred_element_...  36.7 us
    reduce_sum x1, other arithmetic, body(): jnp.sum(weights.astype(jnp.float32) * weights_d.astype(jnp.float32), axis=1)  20.3 us
  transfers between devices with their start and end apart: 28, of which 13 were waited for; matrix products, arithmetic and copies ran while one was open for 41% of the time, Pallas kernels for 5%

profile of v2, /device:TPU:0, one launch (start us, length us, event | category | flops | bytes accessed | tf_op | source)
XLA Modules:
  0.0 700.7 jit_solution(8826865928306071462)
XLA Ops:
  18.6 17.7 %pad_maximum_fusion = bf16[8192,1536]{1,0:T(8,128)(2,1)} fusion(bf16[8192,256]{1,0:T(8,128)(2,1)} %param.13, bf16[8192,256]{1,0:T(8,128)(2,1)} %param.12, bf16[8192,1024]{1,0:T(8,128)(2,1)} %param.11), kind=kLoop, calls=%fused_computation.2 | loop fusion | flops 75497472 | bytes 50331648 | tf_op jit(solution)/shard_map/concatenate | solution.py:302
  42.6 14.2 %fusion.47 = f32[256,1536]{1,0:T(8,128)} fusion(bf16[256,8192]{1,0:T(8,128)(2,1)S(1)} %pad_maximum_fusion.2, bf16[8192,1536]{1,0:T(8,128)(2,1)} %pad_maximum_fusion), kind=kOutput, calls=%fused_computation.110 | convolution fusion | flops 6442450944 | bytes 30932992 | tf_op jit(solution)/shard_map/dot_general | solution.py:305
  56.8 27.8 %collective-permute-done.8 = bf16[1024,1536]{1,0:T(8,128)(2,1)} collective-permute-done((bf16[1024,1536]{1,0:T(8,128)(2,1)}, bf16[1024,1536]{1,0:T(8,128)(2,1)}, u32[]{:S(2)}, u32[]{:S(2)}) %collective-permute-start.8) | collective-permute-done | bytes 3145760 | tf_op jit(solution)/shard_map/ppermute | solution.py:178
  141.3 37.1 %collective-permute-done = bf16[128,8192]{1,0:T(8,128)(2,1)} collective-permute-done((bf16[128,8192]{1,0:T(8,128)(2,1)S(1)}, bf16[128,8192]{1,0:T(8,128)(2,1)}, u32[]{:S(2)}, u32[]{:S(2)}) %collective-permute-start) | collective-permute-done | bytes 2097184 | tf_op jit(solution)/shard_map/ppermute | solution.py:178
  188.3 21.0 %fusion.46 = (bf16[512,1536]{1,0:T(8,128)(2,1)}, f32[512,1536]{1,0:T(8,128)S(1)}) fusion(bf16[512,8192]{1,0:T(8,128)(2,1)S(1)} %pad_maximum_fusion.1, bf16[8192,1536]{1,0:T(8,128)(2,1)} %pad_maximum_fusion), kind=kOutput, calls=%fused_computation.109 | convolution fusion | flops 12885688320 | bytes 38273024 | tf_op jit(solution)/shard_map/dot_general | solution.py:305
  230.0 35.2 %collective-permute-done.7 = bf16[128,8192]{1,0:T(8,128)(2,1)S(1)} collective-permute-done((bf16[128,8192]{1,0:T(8,128)(2,1)}, bf16[128,8192]{1,0:T(8,128)(2,1)S(1)}, u32[]{:S(2)}, u32[]{:S(2)}) %collective-permute-start.7) | collective-permute-done | bytes 2097184 | tf_op jit(solution)/shard_map/ppermute | solution.py:178
  265.5 41.8 %collective-permute-done.5 = bf16[128,8192]{1,0:T(8,128)(2,1)S(1)} collective-permute-done((bf16[128,8192]{1,0:T(8,128)(2,1)}, bf16[128,8192]{1,0:T(8,128)(2,1)S(1)}, u32[]{:S(2)}, u32[]{:S(2)}) %collective-permute-start.5) | collective-permute-done | bytes 2097184 | tf_op jit(solution)/shard_map/ppermute | solution.py:178
  315.2 12.8 %fusion.48 = f32[256,1536]{1,0:T(8,128)S(1)} fusion(bf16[256,8192]{1,0:T(8,128)(2,1)} %copy-done.2, bf16[8192,1536]{1,0:T(8,128)(2,1)} %all-gather.2.cloned.1.call-done), kind=kOutput, calls=%fused_computation.111 | convolution fusion | flops 6442450944 | bytes 30932992 | tf_op jit(solution)/shard_map/dot_general | solution.py:305
  331.4 12.8 %fusion.49 = f32[256,1536]{1,0:T(8,128)S(1)} fusion(bf16[256,8192]{1,0:T(8,128)(2,1)} %copy-done.2, bf16[8192,1536]{1,0:T(8,128)(2,1)} %pad_maximum_fusion), kind=kOutput, calls=%fused_computation.112 | convolution fusion | flops 6442450944 | bytes 30932992 | tf_op jit(solution)/shard_map/dot_general | solution.py:305
  356.3 36.9 %shard_map.118 = (bf16[1024,1024]{1,0:T(8,128)(2,1)}, bf16[1024,1024]{1,0:T(8,128)(2,1)}, bf16[1024,256]{1,0:T(8,128)(2,1)}, bf16[1024,256]{1,0:T(8,128)(2,1)}) custom-call(bf16[1024,1536]{1,0:T(8,128)(2,1)} %select_dynamic-update-slice_fusion.query_ref.key_ref.value_ref, bf16[1024,1536]{1,0:T(8,128)(2,1)} %select_dynamic-update-slice_fusion.query_ref.key_ref.value_ref, ...), custom_call_target="tpu_custom_call" | custom-call | flops 8589934592 | bytes 15728640 | tf_op jit(solution)/shard_map/pallas_call | solution.py:123
  396.7 7.2 %collective-permute-start.10 = (bf16[256,1536]{1,0:T(8,128)(2,1)}, bf16[256,1536]{1,0:T(8,128)(2,1)}, u32[]{:S(2)}, u32[]{:S(2)}) collective-permute-start(bf16[256,1536]{1,0:T(8,128)(2,1)} %get-tuple-element.50), channel_id=1, source_target_pairs={{0,1},{3,2},{4,5},{7,6},{8,9},{11,10},{12,13},{15,14},{16,17},{19,... | collective-permute-start | bytes 2359304 | tf_op jit(solution)/shard_map/ppermute | solution.py:241
  403.9 13.6 %fusion.34 = f32[256,8192]{1,0:T(8,128)} fusion(bf16[8192,1536]{1,0:T(8,128)(2,1)} %pad_maximum_fusion, bf16[1024,1536]{1,0:T(8,128)(2,1)S(1)} %pad_maximum_fusion.5, s32[]{:T(128)S(6)} %select_n.119), kind=kOutput, calls=%fused_computation.54 | convolution fusion | flops 6442450944 | bytes 34340868 | tf_op jit(solution)/shard_map/dot_general | solution.py:48
  417.5 10.8 %fusion.22 = bf16[256,4096]{1,0:T(8,128)(2,1)} fusion(bf16[256,1536]{1,0:T(8,128)(2,1)} %collective-permute-done.10, bf16[8192,1536]{1,0:T(8,128)(2,1)} %all-gather.2.cloned.1.call-done, f32[256,8192]{1,0:T(8,128)} %fusion.34), kind=kOutput, calls=%fused_computation.23 | convolution fusion | flops 3223322624 | bytes 19660800 | tf_op jit(solution)/shard_map/dot_general | solution.py:48
  433.8 36.7 %convolution_convert_fusion = bf16[8192,1536]{1,0:T(8,128)(2,1)} fusion(bf16[1024,8192]{1,0:T(8,128)(2,1)} %fusion.29, bf16[1024,1536]{1,0:T(8,128)(2,1)S(1)} %pad_maximum_fusion.5), kind=kOutput, calls=%fused_computation.1 | convolution fusion | flops 25782386688 | bytes 45088768 | tf_op jit(solution)/shard_map/dot_general | solution.py:42
  476.8 14.4 %fusion.19 = bf16[256,4096]{1,0:T(8,128)(2,1)} fusion(bf16[256,1536]{1,0:T(8,128)(2,1)} %collective-permute-done.10, bf16[8192,1536]{1,0:T(8,128)(2,1)} %all-gather.2.cloned.1.call-done, f32[256,8192]{1,0:T(8,128)} %fusion.34), kind=kOutput, calls=%fused_computation.22 | convolution fusion | flops 3223322624 | bytes 19660800 | tf_op jit(solution)/shard_map/dot_general | solution.py:48
  495.8 22.6 %fusion.30 = f32[512,8192]{1,0:T(8,128)} fusion(bf16[8192,1536]{1,0:T(8,128)(2,1)} %pad_maximum_fusion, bf16[256,1536]{1,0:T(8,128)(2,1)S(1)} %copy-done.17, bf16[256,1536]{1,0:T(8,128)(2,1)S(1)} %copy-done.18), kind=kOutput, calls=%fused_computation.45 | convolution fusion | flops 12888047616 | bytes 43515904 | tf_op jit(solution)/shard_map/dot_general | solution.py:48
  520.8 8.0 %fusion.26 = (bf16[256,4096]{1,0:T(8,128)(2,1)}, bf16[256,4096]{1,0:T(8,128)(2,1)}) fusion(f32[512,8192]{1,0:T(8,128)} %fusion.30, bf16[256,4096]{1,0:T(8,128)(2,1)} %collective-permute-done.12, bf16[256,4096]{1,0:T(8,128)(2,1)S(1)} %collective-permute-done.11), kind=kLoop, calls=%fused_computation.29 | loop fusion | flops 6291456 | bytes 16777216 | tf_op jit(solution)/shard_map/convert_element_type | solution.py:265
  528.8 6.9 collective-permute-start.13
  537.0 28.8 %collective-permute-done.17 = bf16[256,4096]{1,0:T(8,128)(2,1)} collective-permute-done((bf16[256,4096]{1,0:T(8,128)(2,1)}, bf16[256,4096]{1,0:T(8,128)(2,1)}, u32[]{:S(2)}, u32[]{:S(2)}) %collective-permute-start.17) | collective-permute-done | bytes 2097184 | tf_op jit(solution)/shard_map/ppermute | solution.py:178
  572.0 7.4 %collective-permute-start.19 = (bf16[256,4096]{1,0:T(8,128)(2,1)}, bf16[256,4096]{1,0:T(8,128)(2,1)}, u32[]{:S(2)}, u32[]{:S(2)}) collective-permute-start(bf16[256,4096]{1,0:T(8,128)(2,1)} %get-tuple-element.38), channel_id=1, source_target_pairs={{0,1},{1,2},{2,3},{4,5},{5,6},{6,7},{8,9},{9,10},{10,11},{12,13},{... | collective-permute-start | bytes 6291464 | tf_op jit(solution)/shard_map/ppermute | solution.py:178
  580.9 20.3 %multiply_reduce_fusion = f32[8192]{0:T(1024)S(1)} fusion(bf16[8192,1536]{1,0:T(8,128)(2,1)} %convolution_convert_fusion, bf16[8192,1536]{1,0:T(8,128)(2,1)} %pad_maximum_fusion), kind=kLoop, calls=%fused_computation | loop fusion | flops 50323456 | bytes 50364416 | tf_op jit(solution)/shard_map/reduce_sum | solution.py:368
  615.5 36.3 %collective-permute-done.24 = f32[8192]{0:T(1024)S(1)} collective-permute-done((f32[8192]{0:T(1024)S(1)}, f32[8192]{0:T(1024)S(1)}, u32[]{:S(2)}, u32[]{:S(2)}) %collective-permute-start.24) | collective-permute-done | bytes 32800 | tf_op jit(solution)/shard_map/ppermute | solution.py:157
  653.0 13.8 %fusion.36 = f32[256,8192]{1,0:T(8,128)} fusion(bf16[8192,1536]{1,0:T(8,128)(2,1)} %pad_maximum_fusion, bf16[1024,1536]{1,0:T(8,128)(2,1)} %copy-done.10, s32[]{:T(128)S(6)} %select_n.102), kind=kOutput, calls=%fused_computation.56 | convolution fusion | flops 6442450944 | bytes 34340868 | tf_op jit(solution)/shard_map/dot_general | solution.py:48
  667.4 11.1 %fusion.28 = (f32[256,4096]{1,0:T(8,128)}, f32[256,4096]{1,0:T(8,128)}) fusion(f32[256,8192]{1,0:T(8,128)} %fusion.36, bf16[256,4096]{1,0:T(8,128)(2,1)} %collective-permute-done.14, bf16[256,4096]{1,0:T(8,128)(2,1)S(1)} %collective-permute-done.13, bf16[256,4096]{1,0:T(8,128)(2,1)} %collective-permute-done.20, bf16[256,4096]{1,0:T(8,128)(2,1)} %collective-permute-done.19), kind=kLoop, calls=%fused_computation.33 | loop fusion | flops 8388608 | bytes 25165824 | tf_op jit(solution)/shard_map/add | solution.py:234
  (196 shorter events, 190.5 us)
Async XLA Ops:
  7.2 308.0 %all-gather.2.cloned.1.call-start = ((), (), s32[]{:S(2)}) async-start(), calls=%async_computation.1 | async-start | bytes 28311552 | tf_op jit(solution)/shard_map/all_gather | solution.py:193
  12.1 72.6 %collective-permute-start.8 = (bf16[1024,1536]{1,0:T(8,128)(2,1)}, bf16[1024,1536]{1,0:T(8,128)(2,1)}, u32[]{:S(2)}, u32[]{:S(2)}) collective-permute-start(bf16[1024,1536]{1,0:T(8,128)(2,1)} %pad_maximum_fusion.4), channel_id=1, source_target_pairs={{0,1},{3,2},{4,5},{7,6},{8,9},{11,10},{12,13},{15,14},{16,17},{19,... | collective-permute-start | bytes 9437192 | tf_op jit(solution)/shard_map/ppermute | solution.py:178
  84.7 603.3 %reduce-scatter.2.cloned.1.call-start = ((), (), s32[]{:S(2)}) async-start(), calls=%async_computation.2 | async-start | bytes 28311552 | tf_op jit(solution)/shard_map/reduce_scatter | solution.py:367
  84.8 54.7 %collective-permute-start.1 = (bf16[128,8192]{1,0:T(8,128)(2,1)}, bf16[128,8192]{1,0:T(8,128)(2,1)}, u32[]{:S(2)}, u32[]{:S(2)}) collective-permute-start(bf16[128,8192]{1,0:T(8,128)(2,1)} %copy-done.11), channel_id=1, source_target_pairs={{0,1},{1,2},{2,3},{4,5},{5,6},{6,7},{8,9},{9,10},{10,11},{12,13},{... | collective-permute-start | bytes 6291464 | tf_op jit(solution)/shard_map/ppermute | solution.py:178
  90.6 50.7 %collective-permute-start.3 = (bf16[128,8192]{1,0:T(8,128)(2,1)}, bf16[128,8192]{1,0:T(8,128)(2,1)}, u32[]{:S(2)}, u32[]{:S(2)}) collective-permute-start(bf16[128,8192]{1,0:T(8,128)(2,1)} %copy-done.11), channel_id=1, source_target_pairs={{1,0},{2,1},{3,2},{5,4},{6,5},{7,6},{9,8},{10,9},{11,10},{13,12},{... | collective-permute-start | bytes 6291464 | tf_op jit(solution)/shard_map/ppermute | solution.py:178
  91.9 86.6 %collective-permute-start = (bf16[128,8192]{1,0:T(8,128)(2,1)S(1)}, bf16[128,8192]{1,0:T(8,128)(2,1)}, u32[]{:S(2)}, u32[]{:S(2)}) collective-permute-start(bf16[128,8192]{1,0:T(8,128)(2,1)S(1)} %get-tuple-element.23), channel_id=1, source_target_pairs={{0,1},{1,2},{2,3},{4,5},{5,6},{6,7},{8,9},{9,10},{10,11},{12,13},{... | collective-permute-start | bytes 6291464 | tf_op jit(solution)/shard_map/ppermute | solution.py:178
  97.8 86.2 %collective-permute-start.2 = (bf16[128,8192]{1,0:T(8,128)(2,1)S(1)}, bf16[128,8192]{1,0:T(8,128)(2,1)}, u32[]{:S(2)}, u32[]{:S(2)}) collective-permute-start(bf16[128,8192]{1,0:T(8,128)(2,1)S(1)} %get-tuple-element.23), channel_id=1, source_target_pairs={{1,0},{2,1},{3,2},{5,4},{6,5},{7,6},{9,8},{10,9},{11,10},{13,12},{... | collective-permute-start | bytes 6291464 | tf_op jit(solution)/shard_map/ppermute | solution.py:178
  213.7 16.3 %collective-permute-start.6 = (bf16[128,8192]{1,0:T(8,128)(2,1)}, bf16[128,8192]{1,0:T(8,128)(2,1)S(1)}, u32[]{:S(2)}, u32[]{:S(2)}) collective-permute-start(bf16[128,8192]{1,0:T(8,128)(2,1)} %collective-permute-done.1), channel_id=1, source_target_pairs={{1,2},{2,3},{5,6},{6,7},{9,10},{10,11},{13,14},{14,15},{17,18},{18... | collective-permute-start | bytes 6291464 | tf_op jit(solution)/shard_map/ppermute | solution.py:178
  214.5 50.7 %collective-permute-start.7 = (bf16[128,8192]{1,0:T(8,128)(2,1)}, bf16[128,8192]{1,0:T(8,128)(2,1)S(1)}, u32[]{:S(2)}, u32[]{:S(2)}) collective-permute-start(bf16[128,8192]{1,0:T(8,128)(2,1)} %collective-permute-done.3), channel_id=1, source_target_pairs={{1,0},{2,1},{5,4},{6,5},{9,8},{10,9},{13,12},{14,13},{17,16},{18,1... | collective-permute-start | bytes 6291464 | tf_op jit(solution)/shard_map/ppermute | solution.py:178
  215.8 49.6 %collective-permute-start.4 = (bf16[128,8192]{1,0:T(8,128)(2,1)}, bf16[128,8192]{1,0:T(8,128)(2,1)S(1)}, u32[]{:S(2)}, u32[]{:S(2)}) collective-permute-start(bf16[128,8192]{1,0:T(8,128)(2,1)} %collective-permute-done), channel_id=1, source_target_pairs={{1,2},{2,3},{5,6},{6,7},{9,10},{10,11},{13,14},{14,15},{17,18},{18... | collective-permute-start | bytes 6291464 | tf_op jit(solution)/shard_map/ppermute | solution.py:178
  216.6 90.7 %collective-permute-start.5 = (bf16[128,8192]{1,0:T(8,128)(2,1)}, bf16[128,8192]{1,0:T(8,128)(2,1)S(1)}, u32[]{:S(2)}, u32[]{:S(2)}) collective-permute-start(bf16[128,8192]{1,0:T(8,128)(2,1)} %collective-permute-done.2), channel_id=1, source_target_pairs={{1,0},{2,1},{5,4},{6,5},{9,8},{10,9},{13,12},{14,13},{17,16},{18,1... | collective-permute-start | bytes 6291464 | tf_op jit(solution)/shard_map/ppermute | solution.py:178
  311.2 117.1 %collective-permute-start.15 = (bf16[64,8192]{1,0:T(8,128)(2,1)}, bf16[64,8192]{1,0:T(8,128)(2,1)}, u32[]{:S(2)}, u32[]{:S(2)}) collective-permute-start(bf16[64,8192]{1,0:T(8,128)(2,1)} %slice.206), channel_id=1, source_target_pairs={{1,0},{2,3},{5,4},{6,7},{9,8},{10,11},{13,12},{14,15},{17,16},{18,... | collective-permute-start | bytes 3145736 | tf_op jit(solution)/shard_map/ppermute | solution.py:178
  330.1 22.5 %collective-permute-start.9 = (bf16[256,1536]{1,0:T(8,128)(2,1)S(1)}, bf16[256,1536]{1,0:T(8,128)(2,1)}, u32[]{:S(2)}, u32[]{:S(2)}) collective-permute-start(bf16[256,1536]{1,0:T(8,128)(2,1)S(1)} %pad_maximum_fusion.6), channel_id=1, source_target_pairs={{1,0},{2,3},{5,4},{6,7},{9,8},{10,11},{13,12},{14,15},{17,16},{18,... | collective-permute-start | bytes 2359304 | tf_op jit(solution)/shard_map/ppermute | solution.py:329
  352.6 75.7 %collective-permute-start.16 = (bf16[192,8192]{1,0:T(8,128)(2,1)}, bf16[192,8192]{1,0:T(8,128)(2,1)}, u32[]{:S(2)}, u32[]{:S(2)}) collective-permute-start(bf16[192,8192]{1,0:T(8,128)(2,1)} %slice.207), channel_id=1, source_target_pairs={{1,0},{2,3},{5,4},{6,7},{9,8},{10,11},{13,12},{14,15},{17,16},{18,... | collective-permute-start | bytes 9437192 | tf_op jit(solution)/shard_map/ppermute | solution.py:178
  396.7 20.8 %collective-permute-start.10 = (bf16[256,1536]{1,0:T(8,128)(2,1)}, bf16[256,1536]{1,0:T(8,128)(2,1)}, u32[]{:S(2)}, u32[]{:S(2)}) collective-permute-start(bf16[256,1536]{1,0:T(8,128)(2,1)} %get-tuple-element.50), channel_id=1, source_target_pairs={{0,1},{3,2},{4,5},{7,6},{8,9},{11,10},{12,13},{15,14},{16,17},{19,... | collective-permute-start | bytes 2359304 | tf_op jit(solution)/shard_map/ppermute | solution.py:241
  470.5 50.3 %collective-permute-start.11 = (bf16[256,4096]{1,0:T(8,128)(2,1)}, bf16[256,4096]{1,0:T(8,128)(2,1)S(1)}, u32[]{:S(2)}, u32[]{:S(2)}) collective-permute-start(bf16[256,4096]{1,0:T(8,128)(2,1)} %fusion.22), channel_id=1, source_target_pairs={{0,1},{1,2},{4,5},{5,6},{8,9},{9,10},{12,13},{13,14},{16,17},{17,1... | collective-permute-start | bytes 6291464 | tf_op jit(solution)/shard_map/ppermute | solution.py:178
  474.6 46.2 %collective-permute-start.12 = (bf16[256,4096]{1,0:T(8,128)(2,1)}, bf16[256,4096]{1,0:T(8,128)(2,1)}, u32[]{:S(2)}, u32[]{:S(2)}) collective-permute-start(bf16[256,4096]{1,0:T(8,128)(2,1)} %fusion.22), channel_id=1, source_target_pairs={{2,1},{3,2},{6,5},{7,6},{10,9},{11,10},{14,13},{15,14},{18,17},{19... | collective-permute-start | bytes 6291464 | tf_op jit(solution)/shard_map/ppermute | solution.py:178
  491.2 74.6 %collective-permute-start.17 = (bf16[256,4096]{1,0:T(8,128)(2,1)}, bf16[256,4096]{1,0:T(8,128)(2,1)}, u32[]{:S(2)}, u32[]{:S(2)}) collective-permute-start(bf16[256,4096]{1,0:T(8,128)(2,1)} %fusion.19), channel_id=1, source_target_pairs={{0,1},{1,2},{4,5},{5,6},{8,9},{9,10},{12,13},{13,14},{16,17},{17,1... | collective-permute-start | bytes 6291464 | tf_op jit(solution)/shard_map/ppermute | solution.py:178
  493.8 72.0 %collective-permute-start.18 = (bf16[256,4096]{1,0:T(8,128)(2,1)}, bf16[256,4096]{1,0:T(8,128)(2,1)}, u32[]{:S(2)}, u32[]{:S(2)}) collective-permute-start(bf16[256,4096]{1,0:T(8,128)(2,1)} %fusion.19), channel_id=1, source_target_pairs={{2,1},{3,2},{6,5},{7,6},{10,9},{11,10},{14,13},{15,14},{18,17},{19... | collective-permute-start | bytes 6291464 | tf_op jit(solution)/shard_map/ppermute | solution.py:178
  528.8 138.6 %collective-permute-start.13 = (bf16[256,4096]{1,0:T(8,128)(2,1)}, bf16[256,4096]{1,0:T(8,128)(2,1)S(1)}, u32[]{:S(2)}, u32[]{:S(2)}) collective-permute-start(bf16[256,4096]{1,0:T(8,128)(2,1)} %get-tuple-element.32), channel_id=1, source_target_pairs={{0,1},{1,2},{2,3},{4,5},{5,6},{6,7},{8,9},{9,10},{10,11},{12,13},{... | collective-permute-start | bytes 6291464 | tf_op jit(solution)/shard_map/ppermute | solution.py:178
  535.7 131.8 %collective-permute-start.14 = (bf16[256,4096]{1,0:T(8,128)(2,1)}, bf16[256,4096]{1,0:T(8,128)(2,1)}, u32[]{:S(2)}, u32[]{:S(2)}) collective-permute-start(bf16[256,4096]{1,0:T(8,128)(2,1)} %get-tuple-element.33), channel_id=1, source_target_pairs={{1,0},{2,1},{3,2},{5,4},{6,5},{7,6},{9,8},{10,9},{11,10},{13,12},{... | collective-permute-start | bytes 6291464 | tf_op jit(solution)/shard_map/ppermute | solution.py:178
  572.0 95.4 %collective-permute-start.19 = (bf16[256,4096]{1,0:T(8,128)(2,1)}, bf16[256,4096]{1,0:T(8,128)(2,1)}, u32[]{:S(2)}, u32[]{:S(2)}) collective-permute-start(bf16[256,4096]{1,0:T(8,128)(2,1)} %get-tuple-element.38), channel_id=1, source_target_pairs={{0,1},{1,2},{2,3},{4,5},{5,6},{6,7},{8,9},{9,10},{10,11},{12,13},{... | collective-permute-start | bytes 6291464 | tf_op jit(solution)/shard_map/ppermute | solution.py:178
  579.4 88.0 %collective-permute-start.20 = (bf16[256,4096]{1,0:T(8,128)(2,1)}, bf16[256,4096]{1,0:T(8,128)(2,1)}, u32[]{:S(2)}, u32[]{:S(2)}) collective-permute-start(bf16[256,4096]{1,0:T(8,128)(2,1)} %get-tuple-element.39), channel_id=1, source_target_pairs={{1,0},{2,1},{3,2},{5,4},{6,5},{7,6},{9,8},{10,9},{11,10},{13,12},{... | collective-permute-start | bytes 6291464 | tf_op jit(solution)/shard_map/ppermute | solution.py:178
  612.1 39.7 %collective-permute-start.24 = (f32[8192]{0:T(1024)S(1)}, f32[8192]{0:T(1024)S(1)}, u32[]{:S(2)}, u32[]{:S(2)}) collective-permute-start(f32[8192]{0:T(1024)S(1)} %add.184), channel_id=1, source_target_pairs={{0,1},{1,0},{2,3},{3,2},{4,5},{5,4},{6,7},{7,6},{8,9},{9,8},{10,11... | collective-permute-start | bytes 98312 | tf_op jit(solution)/shard_map/ppermute | solution.py:157
  (36 other events, 413.6 us)
Sparse Core Ops, SparseCore 0:
  84.8 126.3 all-gather.1
  470.6 156.3 reduce-scatter.1
